TPU v7x, 256 devices: a whole 4x4x8 slice. The times are simulated.
256 devices in a mesh: seq: 8 (over z), chan: 32 (over y, x, core).
Axes of the slice: x: 4, y: 4, z: 8, core: 2. Of those that a mesh axis runs over, the one named last changes fastest.
Arguments:
- tokens: bfloat16 [8192, 4096], P('seq', 'chan'), may hold values from -8 to 8
- norm_gain: float32 [4096], replicated, may hold values from 0.5 to 1.5
- gate_proj: bfloat16 [4096, 8192], P(None, 'chan'), may hold values from -0.09375 to 0.09375
- inner_proj: bfloat16 [4096, 8192], P(None, 'chan'), may hold values from -0.09375 to 0.09375
- state_proj: bfloat16 [4096, 384], P('chan'), may hold values from -0.11816406 to 0.11816406
- conv_inner: float32 [4, 8192], P(None, 'chan'), may hold values from -3 to 3
- conv_state: float32 [4, 256], replicated, may hold values from -3 to 3
- log_rate: float32 [128], P('chan'), may hold values from -1 to 0
- rate_bias: float32 [128], P('chan'), may hold values from -16 to -2
- skip_gain: float32 [128], P('chan'), may hold values from 0.2 to 4
- gate_gain: float32 [8192], P('chan'), may hold values from 0.5 to 1.5
- out_proj: bfloat16 [8192, 4096], P('chan'), may hold values from -0.125 to 0.125
Outputs:
- layer_out: bfloat16 [8192, 4096], P('seq', 'chan')
All inputs are finite; a program needn't handle non-finite values.
Results may differ from a plain program's by a relative error of at most 0.012.
Values may be sent and summed in bfloat16 or wider, within the bound.
A program may use at most 128 MiB of HBM per device.

v0:
```python
import jax
import jax.numpy as jnp
from jax import lax
from jax.sharding import PartitionSpec as P

P_SIZE = 64
N = 128
K = 4
Q = 256
DI = 8192


def from_behind(value, axis, steps):
    count = lax.axis_size(axis)
    leading, last = (max(0, -steps), min(count, count - steps))
    return lax.ppermute(value, axis, [(source, source + steps) for source in range(leading, last)])


def prefix(value, axis, join, neutral):
    count, mine = (lax.axis_size(axis), lax.axis_index(axis))
    pieces = jax.tree.map(lambda part: lax.all_gather(part, axis), value)
    total = jax.tree.map(
        lambda part, zero: jnp.full_like(part, 0) + jnp.asarray(zero, part.dtype), value, neutral
    )

    def turn(position, total):
        longer = join(total, jax.tree.map(lambda part: part[position], pieces))
        return jax.tree.map(lambda new, old: jnp.where(position < mine, new, old), longer, total)

    return lax.fori_loop(0, count - 1, turn, total)


def from_everyone(x, axis):
    size = lax.axis_size(axis)
    return lax.all_to_all(jnp.broadcast_to(x[None], (size, *x.shape)), axis, 0, 0, tiled=True)


def over_copies(x, axis):
    everything = from_everyone(x, axis)
    return jnp.sum(everything, axis=0)


def causal_mix(rim_part, fresh_rows, weights):
    length = fresh_rows.shape[0]
    padded = jnp.concatenate([rim_part.astype(jnp.float32), fresh_rows.astype(jnp.float32)], axis=0)
    summed = jnp.zeros(fresh_rows.shape, jnp.float32)
    for offset in range(weights.shape[0]):
        summed = summed + weights[offset] * padded[offset : offset + length]
    return jax.nn.silu(summed)


def combine_pair(earlier_part, later_part):
    return (
        earlier_part[0] * later_part[0],
        later_part[0][:, None, None] * earlier_part[1] + later_part[1],
    )


def local(
    tokens,
    norm_gain,
    gate_proj,
    inner_proj,
    state_proj,
    conv_inner,
    conv_state,
    log_rate,
    rate_bias,
    skip_gain,
    gate_gain,
    out_proj,
):
    gathered = lax.all_gather(tokens, "chan", axis=1, tiled=True)
    widened = gathered.astype(jnp.float32)
    inverse = lax.rsqrt(jnp.mean(widened * widened, axis=1, keepdims=True) + 1e-05)
    normed = (widened * inverse * norm_gain).astype(jnp.bfloat16)
    gate_raw = jnp.dot(normed, gate_proj, preferred_element_type=jnp.float32).astype(jnp.bfloat16)
    inner_raw = jnp.dot(normed, inner_proj, preferred_element_type=jnp.float32).astype(jnp.bfloat16)
    heads = log_rate.shape[0]
    start_head = lax.axis_index("chan") * heads
    projected = jnp.dot(
        normed,
        lax.all_gather(state_proj, "chan", axis=0, tiled=True),
        preferred_element_type=jnp.float32,
    )
    state_raw = projected[:, : 2 * N]
    raw_rate = lax.dynamic_slice_in_dim(projected, 2 * N + start_head, heads, 1)
    rim_rows = from_behind(
        (inner_raw[-(K - 1) :].astype(jnp.float32), state_raw[-(K - 1) :]), "seq", 1
    )
    inner_conv = causal_mix(rim_rows[0].astype(jnp.bfloat16), inner_raw, conv_inner)
    state_conv = causal_mix(rim_rows[1], state_raw, conv_state)
    token_rows = tokens.shape[0]
    blocks = token_rows // Q
    step_size = jax.nn.softplus(raw_rate + rate_bias)
    decay_log = -jnp.exp(log_rate) * step_size
    values = inner_conv.reshape(blocks, Q, heads, P_SIZE)
    in_map = state_conv[:, :N].reshape(blocks, Q, N)
    out_map = state_conv[:, N:].reshape(blocks, Q, N)
    step_rows = step_size.reshape(blocks, Q, heads).transpose(0, 2, 1)
    log_rows = decay_log.reshape(blocks, Q, heads).transpose(0, 2, 1)
    lower_mask = (jnp.arange(Q)[:, None] >= jnp.arange(Q)[None, :]).astype(jnp.float32)
    within = jnp.einsum("chs,ts->cht", log_rows, lower_mask)
    log_gaps = within[..., :, None] - within[..., None, :]
    fading = jnp.exp(jnp.where(lower_mask > 0, log_gaps, -jnp.inf))
    scores = jnp.einsum("ctn,csn->cts", out_map, in_map)
    mixing = scores[:, None] * fading * step_rows[:, :, None, :]
    local_out = jnp.einsum("chts,cshp->cthp", mixing, values)
    tail_weight = jnp.exp(within[..., -1:] - within) * step_rows
    scaled = values * tail_weight.transpose(0, 2, 1)[..., None]
    block_end = jnp.einsum("csn,cshp->chnp", in_map, scaled)
    block_log = within[..., -1]
    through = jnp.cumsum(block_log, axis=0)
    before = through - block_log
    earlier = jnp.arange(blocks)[:, None] > jnp.arange(blocks)[None, :]
    passage = jnp.exp(
        jnp.where(earlier[:, :, None], before[:, None, :] - through[None, :, :], -jnp.inf)
    )
    entering = jnp.einsum("cdh,dhnp->chnp", passage, block_end)
    device_end = jnp.einsum("ch,chnp->hnp", jnp.exp(through[-1:] - through), block_end)
    device_fade = jnp.exp(through[-1])
    identity = (jnp.ones_like(device_fade), jnp.zeros_like(device_end))
    carried = prefix((device_fade, device_end), "seq", combine_pair, identity)[1]
    entering = entering + jnp.exp(before)[:, :, None, None] * carried[None]
    carried_out = jnp.einsum("ctn,chnp->cthp", out_map, entering)
    carried_out = carried_out * jnp.exp(within).transpose(0, 2, 1)[..., None]
    skip_wide = jnp.repeat(skip_gain, P_SIZE)
    ssd_out = (local_out + carried_out).reshape(token_rows, heads * P_SIZE) + skip_wide * inner_conv
    gated_out = ssd_out * jax.nn.silu(gate_raw.astype(jnp.float32))
    energy = over_copies(jnp.sum(gated_out * gated_out, axis=1), "chan")
    norm_scale = lax.rsqrt(energy / DI + 1e-05)
    shaped = (gated_out * norm_scale[:, None] * gate_gain).astype(jnp.bfloat16)
    column_rows = lax.all_to_all(out_proj, "chan", split_axis=1, concat_axis=0, tiled=True)
    summed = jnp.dot(
        lax.all_gather(shaped, "chan", axis=1, tiled=True),
        column_rows,
        preferred_element_type=jnp.float32,
    )
    return (tokens.astype(jnp.float32) + summed).astype(jnp.bfloat16)


def solution(mesh):
    return jax.shard_map(
        local,
        mesh=mesh,
        in_specs=(
            P("seq", "chan"),
            P(),
            P(None, "chan"),
            P(None, "chan"),
            P("chan", None),
            P(None, "chan"),
            P(),
            P("chan"),
            P("chan"),
            P("chan"),
            P("chan"),
            P("chan", None),
        ),
        out_specs=P("seq", "chan"),
        check_vma=False,
    )
```

profile of v0, /device:TPU:2, one launch (start us, length us, event | category | flops | bytes accessed | tf_op | source)
XLA Modules:
  0.0 362.4 jit_solution(8693260345117643009)
XLA Ops:
  6.5 0.7 all-gather.7.cloned.1.call-update
  7.3 0.7 all-gather.9.cloned.1.call-update
  8.1 0.7 exponential_negate_fusion
  8.7 0.8 fusion.68
  9.6 0.8 fusion.69
  10.4 65.9 %all-gather.7.cloned.1.call-done = bf16[1024,4096]{1,0:T(8,128)(2,1)} async-done(((bf16[1024,128]{1,0:T(8,128)(2,1)}), bf16[1024,4096]{1,0:T(8,128)(2,1)}) %all-gather.7.cloned.1.call-update) | async-done | bytes 8388624 | tf_op jit(solution)/shard_map/all_gather | solution.py:73
  76.3 5.1 %fusion.1 = f32[1024]{0:T(1024)S(1)} fusion(bf16[1024,4096]{1,0:T(8,128)(2,1)} %all-gather.7.cloned.1.call-done), kind=kLoop, calls=%fused_computation.6 | loop fusion | flops 12581888 | bytes 8392704 | tf_op jit(solution)/shard_map/reduce_sum | solution.py:75
  81.4 46.9 %all-gather.9.cloned.1.call-done = bf16[4096,384]{1,0:T(8,128)(2,1)} async-done(((bf16[128,384]{1,0:T(8,128)(2,1)}), bf16[4096,384]{1,0:T(8,128)(2,1)}) %all-gather.9.cloned.1.call-update) | async-done | bytes 3145744 | tf_op jit(solution)/shard_map/all_gather | solution.py:83
  128.3 8.1 %fusion.63 = f32[1024,384]{1,0:T(8,128)S(1)} fusion(bf16[4096,384]{1,0:T(8,128)(2,1)} %all-gather.9.cloned.1.call-done, bf16[1024,4096]{1,0:T(8,128)(2,1)} %all-gather.7.cloned.1.call-done, f32[4096]{0:T(1024)S(1)} %copy-done.10, f32[1024]{0:T(1024)S(1)} %add_rsqrt_fusion.1), kind=kOutput, calls=%fused_computation.97 | convolution fusion | flops 3238002688 | bytes 13127680 | tf_op jit(solution)/shard_map/dot_general | solution.py:81
  136.4 3.5 collective-permute-start.1
  139.9 0.2 constant_dynamic-slice_fusion.1
  140.1 0.2 copy.156
  140.3 0.1 broadcast_multiply_fusion.1
  140.4 0.2 fusion.50
  140.6 0.2 slice_reduce_fusion
  140.9 5.9 %fusion.70 = (f32[1024,256]{1,0:T(8,128)S(1)}, bf16[1024,256]{1,0:T(8,128)(2,1)S(1)}) fusion(bf16[4096,256]{1,0:T(8,128)(2,1)S(1)} %copy-done, bf16[1024,4096]{1,0:T(8,128)(2,1)} %all-gather.7.cloned.1.call-done, f32[4096]{0:T(1024)S(1)} %copy-done.10, f32[1024]{0:T(1024)S(1)} %add_rsqrt_fusion.1), kind=kOutput, calls=%fused_computation.102 | convolution fusion | flops 2164785152 | bytes 12079104 | tf_op jit(solution)/shard_map/dot_general | solution.py:78
  146.8 3.5 collective-permute-start
  150.3 1.1 slice.93
  151.4 0.2 collective-permute-done
  151.6 0.6 divide_multiply_fusion.1
  152.2 1.3 copy.120
  153.6 2.8 reshape.81
  156.3 1.4 broadcast_multiply_fusion
  157.8 3.1 divide_multiply_fusion
  161.0 0.7 copy-done.5
  161.7 0.9 fusion.47
  163.2 16.8 %all-gather.1 = f32[8,1,4]{2,1,0:T(1,128)S(1)} all-gather(f32[1,1,4]{2,1,0:T(1,128)S(1)} %get-tuple-element.179), channel_id=1, replica_groups=mesh['seq'=8,'chan'=32] {'seq'}, dimensions={0}, use_global_device_ids=true | all-gather | bytes 144 | tf_op jit(solution)/shard_map/all_gather | solution.py:21
  180.0 2.2 fusion.71
  182.3 19.9 %all-gather.13.cloned.1.call-done = f32[32,128,64]{1,2,0:T(8,128)} async-done(((f32[4,128,64]{1,2,0:T(8,128)}), f32[32,128,64]{1,2,0:T(8,128)}) %all-gather.13.cloned.1.call-update) | async-done | bytes 1048592 | tf_op jit(solution)/shard_map/all_gather | solution.py:21
  202.1 8.4 %while.14 = (s32[]{:T(128)}, f32[4,128,64]{2,1,0:T(8,128)S(1)}, s32[]{:T(128)}, f32[8,4]{1,0:T(8,128)S(1)}, f32[8,4,128,64]{2,3,1,0:T(8,128)}, /*index=5*/s32[]{:T(128)}, s32[]{:T(128)}) while((s32[]{:T(128)}, f32[4,128,64]{2,1,0:T(8,128)S(1)}, s32[]{:T(128)}, f32[8,4]{1,0:T(8,128)S(1)}, f32[8,4,128,64]{2,3,1,0:T(8,128)}, ...), condition=%wide.region_3.4_spmd.clone, body=%wide.region_2.3_spmd.clone.sunk | while | flops 131076 | bytes 917665 | solution.py:30
  202.1 0.9 constant_dynamic-slice_fusion.3
  203.1 0.1 copy.166
  203.2 0.1 fusion.85
  203.3 0.9 constant_dynamic-slice_fusion.3
  204.3 0.1 copy.166
  204.4 0.1 fusion.85
  204.5 0.9 constant_dynamic-slice_fusion.3
  205.5 0.1 copy.166
  205.6 0.1 fusion.85
  205.7 0.9 constant_dynamic-slice_fusion.3
  206.7 0.1 copy.166
  206.8 0.1 fusion.85
  206.9 0.9 constant_dynamic-slice_fusion.3
  207.9 0.1 copy.166
  208.0 0.1 fusion.85
  208.2 0.9 constant_dynamic-slice_fusion.3
  209.1 0.1 copy.166
  209.2 0.1 fusion.85
  209.4 0.9 constant_dynamic-slice_fusion.3
  210.3 0.1 copy.166
  210.5 0.1 copy.135
  210.6 0.4 fusion.22
  211.1 0.3 fusion.72
  211.4 3.9 %fusion.19 = f32[4,256,4,64]{1,3,2,0:T(8,128)} fusion(f32[4,4,256]{2,1,0:T(4,128)S(1)} %copy.123, f32[4,4,256]{2,1,0:T(4,128)S(1)} %fusion.50, f32[4,256,256]{2,1,0:T(8,128)} %fusion.71, pred[256,256]{1,0:T(8,128)(4,1)S(1)} %convert_compare_fusion, f32[4,256,4,64]{1,0,3,2:T(4,128)} %reshape.81, f32[4,256,4,64]{1,3,2,0:T(8,128)S(1)} %bitcast.90, ...), kind=kOutput, calls=%fused_computation.26 | convolution fusion | flops 138936320 | bytes 4308992 | tf_op jit(solution)/shard_map/chts,cshp->cthp/dot_general | solution.py:108
  215.3 2.9 copy.152
  218.1 3.2 reshape.97
  221.4 7.8 %multiply_reduce_fusion = (f32[1024]{0:T(1024)S(1)}, f32[1024,256]{1,0:T(8,128)}) fusion(bf16[4096,256]{1,0:T(8,128)(2,1)} %param.16, bf16[1024,4096]{1,0:T(8,128)(2,1)} %all-gather.7.cloned.1.call-done, f32[4096]{0:T(1024)S(1)} %copy-done.10, f32[1024]{0:T(1024)S(1)} %add_rsqrt_fusion.1, f32[1024,256]{1,0:T(8,128)} %reshape.97, ...), kind=kOutput, calls=%fused_computation.61 | convolution fusion | flops 2167143424 | bytes 13657088 | tf_op jit(solution)/shard_map/dot_general | solution.py:77
  229.2 13.8 %all_to_all.25 = f32[32,1,1024]{2,1,0:T(1,128)S(1)} all-to-all(f32[32,1,1024]{2,1,0:T(1,128)S(1)} %broadcast_in_dim.32), channel_id=1, replica_groups=mesh['seq'=8,'chan'=32] {'chan'}, dimensions={0} | all-to-all | bytes 262144 | tf_op jit(solution)/shard_map/all_to_all | solution.py:35
  243.1 2.2 multiply_convert_fusion
  245.4 4.1 %copy.141 = bf16[256,4096]{0,1:T(8,128)(2,1)} copy(bf16[256,4096]{1,0:T(8,128)(2,1)} %param.25) | data formatting | bytes 4194304 | tf_op args[11]
  249.5 40.9 %all_to_all.26 = bf16[256,32,128]{0,2,1:T(8,128)(2,1)} all-to-all(bf16[256,32,128]{0,2,1:T(8,128)(2,1)} %bitcast.86), channel_id=1, replica_groups=mesh['seq'=8,'chan'=32] {'chan'}, dimensions={1} | all-to-all | bytes 4194304 | tf_op jit(solution)/shard_map/all_to_all | solution.py:133
  290.3 4.1 %copy.142 = bf16[32,256,128]{2,1,0:T(8,128)(2,1)} copy(bf16[32,256,128]{1,2,0:T(8,128)(2,1)} %bitcast.85) | data formatting | bytes 4194304 | tf_op jit(solution)/shard_map/all_to_all | solution.py:133
  294.4 49.9 %all-gather.11.cloned.1.call-done = bf16[1024,8192]{1,0:T(8,128)(2,1)} async-done(((bf16[1024,256]{1,0:T(8,128)(2,1)}), bf16[1024,8192]{1,0:T(8,128)(2,1)}) %all-gather.11.cloned.1.call-update) | async-done | bytes 16777232 | tf_op jit(solution)/shard_map/all_gather | solution.py:135
  344.3 11.6 %fusion.23 = bf16[1024,128]{1,0:T(8,128)(2,1)} fusion(bf16[1024,8192]{1,0:T(8,128)(2,1)} %all-gather.11.cloned.1.call-done, bf16[8192,128]{1,0:T(8,128)(2,1)} %bitcast.89, bf16[1024,128]{1,0:T(8,128)(2,1)S(1)} %copy-done.6), kind=kOutput, calls=%fused_computation.34 | convolution fusion | flops 2147876864 | bytes 19398656 | tf_op jit(solution)/shard_map/dot_general | solution.py:134
  (61 shorter events, 1.3 us)
Async XLA Ops:
  6.5 134.3 %copy-start = (bf16[4096,256]{1,0:T(8,128)(2,1)S(1)}, bf16[4096,256]{1,0:T(8,128)(2,1)}, u32[]{:S(2)}) copy-start(bf16[4096,256]{1,0:T(8,128)(2,1)} %param.17) | copy-start | bytes 6291460
  6.5 69.7 %all-gather.7.cloned.1.call-start = ((), (), s32[]{:S(2)}) async-start(), calls=%async_computation.2 | async-start | bytes 8650752 | tf_op jit(solution)/shard_map/all_gather | solution.py:73
  7.3 121.0 %all-gather.9.cloned.1.call-start = ((), (), s32[]{:S(2)}) async-start(), calls=%async_computation.3 | async-start | bytes 3244032 | tf_op jit(solution)/shard_map/all_gather | solution.py:83
  8.0 194.1 %all-gather.13.cloned.1.call-start = ((), (), s32[]{:S(2)}) async-start(), calls=%async_computation.5 | async-start | bytes 1179648 | tf_op jit(solution)/shard_map/all_gather | solution.py:21
  10.4 117.9 %copy-start.10 = (f32[4096]{0:T(1024)S(1)}, f32[4096]{0:T(1024)}, u32[]{:S(2)}) copy-start(f32[4096]{0:T(1024)} %param.15) | copy-start | bytes 49156
  81.4 58.9 %copy-start.8 = (f32[4]{0:T(128)S(1)}, f32[4]{0:T(128)}, u32[]{:S(2)}) copy-start(f32[4]{0:T(128)} %param.22) | copy-start | bytes 52
  136.4 3.5 copy-start.3
  136.4 21.4 %collective-permute-start.1 = (f32[3,256]{1,0:T(4,128)S(1)}, f32[3,256]{1,0:T(4,128)S(1)}, u32[]{:S(2)}, u32[]{:S(2)}) collective-permute-start(f32[3,256]{1,0:T(4,128)S(1)} %slice.92), channel_id=1, source_target_pairs={{0,32},{32,64},{64,96},{96,128},{128,160},{160,192},{192,224},{1,3... | collective-permute-start | bytes 9224 | tf_op jit(solution)/shard_map/ppermute | solution.py:16
  140.9 9.4 %copy-start.4 = (f32[1024,384]{1,0:T(8,128)S(1)}, f32[1024,384]{1,0:T(8,128)}, u32[]{:S(2)}) copy-start(f32[1024,384]{1,0:T(8,128)} %copy-done.3) | copy-start | bytes 4718596
  146.8 4.8 %collective-permute-start = (bf16[3,256]{1,0:T(4,128)(2,1)S(1)}, bf16[3,256]{1,0:T(4,128)(2,1)S(1)}, u32[]{:S(2)}, u32[]{:S(2)}) collective-permute-start(bf16[3,256]{1,0:T(4,128)(2,1)S(1)} %slice.161), channel_id=1, source_target_pairs={{0,32},{32,64},{64,96},{96,128},{128,160},{160,192},{192,224},{1,3... | collective-permute-start | bytes 4616 | tf_op jit(solution)/shard_map/ppermute | solution.py:16
  152.2 8.7 %copy-start.1 = (f32[1024,256]{1,0:T(8,128)}, f32[1024,256]{1,0:T(8,128)S(1)}, u32[]{:S(2)}) copy-start(f32[1024,256]{1,0:T(8,128)S(1)} %divide_multiply_fusion.1) | copy-start | bytes 3145732
  153.6 9.1 %copy-start.9 = (f32[4]{0:T(128)S(1)}, f32[4]{0:T(128)}, u32[]{:S(2)}) copy-start(f32[4]{0:T(128)} %param.23) | copy-start | bytes 52
  161.0 0.7 copy-start.5
  162.6 181.6 %all-gather.11.cloned.1.call-start = ((), (), s32[]{:S(2)}) async-start(), calls=%async_computation.4 | async-start | bytes 17301504 | tf_op jit(solution)/shard_map/all_gather | solution.py:135
  215.3 6.1 %copy-start.2 = (f32[1024,256]{1,0:T(8,128)S(1)}, f32[1024,256]{1,0:T(8,128)}, u32[]{:S(2)}) copy-start(f32[1024,256]{1,0:T(8,128)} %copy-done.1) | copy-start | bytes 3145732
  221.3 21.8 %copy-start.7 = (f32[256]{0:T(256)S(1)}, f32[256]{0:T(256)}, u32[]{:S(2)}) copy-start(f32[256]{0:T(256)} %param.24) | copy-start | bytes 3076
  249.5 94.8 %copy-start.6 = (bf16[1024,128]{1,0:T(8,128)(2,1)S(1)}, bf16[1024,128]{1,0:T(8,128)(2,1)}, u32[]{:S(2)}) copy-start(bf16[1024,128]{1,0:T(8,128)(2,1)} %param.14) | copy-start | bytes 786436
Sparse Core Ops, SparseCore 0:
  9.8 66.4 all-gather.6
  78.8 49.4 all-gather.8
  162.8 39.3 all-gather.12
  245.5 98.7 all-gather.10
where the time goes:
time: 365 us; the launch traced here: 362 us
  waiting for transfers between devices  184 us (50%)
  blocking collectives  71.5 us (20%)
  matrix products  41.3 us (11%)
  local copies, waits for them, and re-layouts  30.5 us (8%)
  other arithmetic  14.3 us (4%)
  between operations  13.4 us (4%)
  starting transfers between devices  7.09 us (2%)
    all_gather x1, waiting for transfers between devices, local(): gathered = lax.all_gather(tokens, 'chan', axis=1, tiled=True)  65.9 us
    all_gather x1, waiting for transfers between devices, local(): lax.all_gather(shaped, 'chan', axis=1, tiled=True)  49.9 us
    all_gather x1, waiting for transfers between devices, local(): lax.all_gather(state_proj, 'chan', axis=0, tiled=True)  46.9 us
    all_to_all x1, blocking collectives, local(): lax.all_to_all(out_proj, 'chan', split_axis=1, concat_axis=0, tiled=True)  40.9 us
    all_gather x1, waiting for transfers between devices, prefix(): pieces = jax.tree.map(lambda part: lax.all_gather(part, axis), value)  19.9 us
    all_gather x1, blocking collectives, prefix(): pieces = jax.tree.map(lambda part: lax.all_gather(part, axis), value)  16.8 us
    all_to_all x1, blocking collectives, from_everyone(): lax.all_to_all(jnp.broadcast_to(x[None], (size, *x.shape)), axis, 0, 0, t...  13.8 us
    dot_general x1, matrix products, local(): jnp.dot(lax.all_gather(shaped, 'chan', axis=1, tiled=True), column_rows,...  11.6 us
  transfers between devices with their start and end apart: 6, of which 5 were waited for; matrix products, arithmetic and copies ran while one was open for 9% of the time, Pallas kernels for 0%

commit v1 on v0

v1 whole, which is shorter than its diff:
```python
import functools

import jax
import jax.numpy as jnp
from jax import lax
from jax.experimental import pallas as pl
from jax.experimental.pallas import tpu as pltpu
from jax.sharding import PartitionSpec as P

P_SIZE = 64
N = 128
K = 4
Q = 256
DI = 8192
F32 = jnp.float32
BF = jnp.bfloat16
MESH = pl.DeviceIdType.MESH
HALO = 16
VLIM = 62 * 1024 * 1024


def place():
    c = lax.axis_index("chan")
    k = lax.rem(c, 2)
    chip = c // 2
    return chip // 4, lax.rem(chip, 4), k


def wrap4(v):
    return lax.rem(v + 4, 4)


def chan_id(y, x, k):
    return (wrap4(y) * 4 + wrap4(x)) * 2 + k


def remote(src, dst, send, recv, chan):
    return pltpu.make_async_remote_copy(
        src_ref=src, dst_ref=dst, send_sem=send, recv_sem=recv,
        device_id={"chan": chan}, device_id_type=MESH,
    )


ROWS = 1024
SROWS = 384
GROWS = ROWS + SROWS + HALO
PIECES = [((0, 128), (128, 128)), ((1024, 208), (1232, 192))] + [
    ((q * 256, 128), (q * 256 + 128, 128)) for q in (1, 2, 3)
]
NP = len(PIECES)


def half_rows(n):
    a = (n // 2 + 15) // 16 * 16
    return a, n - a


def gather_kernel(
    tok, stp, gain, gate_hbm, inner_hbm, gate_out, inner_out, proj_out,
    G, X, WsT, Wgi, inv, send, recv, zsem, lsem,
):
    y, x, k = place()
    z = lax.axis_index("seq")

    def peer(axis, d):
        return chan_id(y, x + d, k) if axis == 0 else chan_id(y + d, x, k)

    sib = chan_id(y, x, 1 - k)

    wcopies = [
        pltpu.make_async_copy(gate_hbm, Wgi.at[:, 0:256], lsem.at[0]),
        pltpu.make_async_copy(inner_hbm, Wgi.at[:, 256:512], lsem.at[1]),
    ]
    own = pltpu.make_async_copy(tok, G.at[y, x, k, pl.ds(0, ROWS)], lsem.at[2])
    for cp in wcopies:
        cp.start()
    own.start()

    bar = pltpu.get_barrier_semaphore()
    for d in (sib, peer(0, 1), peer(0, -1), peer(1, 1), peer(1, -1)):
        pl.semaphore_signal(bar, inc=1, device_id={"chan": d}, device_id_type=MESH)
    for dz in (1, 7):
        pl.semaphore_signal(bar, inc=1, device_id={"seq": lax.rem(z + dz, 8)}, device_id_type=MESH)
    pl.semaphore_wait(bar, 7)

    halo = pltpu.make_async_remote_copy(
        src_ref=tok.at[pl.ds(ROWS - HALO, HALO)],
        dst_ref=G.at[y, x, k, pl.ds(ROWS + SROWS, HALO)],
        send_sem=zsem.at[0], recv_sem=zsem.at[1],
        device_id={"seq": lax.rem(z + 1, 8)}, device_id_type=MESH,
    )
    halo.start()

    D = {}

    def go(i, h, e, src, dst, chan):
        cp = remote(src, dst, send.at[i, h, e], recv.at[i, h, e], chan)
        cp.start()
        D[i, h, e] = cp

    def blk(axis, d, r0, n):
        if axis == 0:
            return G.at[y, wrap4(x + d), k, pl.ds(r0, n)]
        return G.at[wrap4(y + d), x, k, pl.ds(r0, n)]

    def line(h, d, r0, n):
        if h == 0:
            return G.at[wrap4(y + d), :, k, pl.ds(r0, n)]
        return G.at[:, wrap4(x + d), k, pl.ds(r0, n)]

    def t0(i):
        for h in (0, 1):
            r0, n = PIECES[i][h]
            src = G.at[y, x, k, pl.ds(r0, n)] if i == 1 else tok.at[pl.ds(r0, n)]
            dst = G.at[y, x, k, pl.ds(r0, n)]
            go(i, h, 0, src, dst, peer(h, 1))
            go(i, h, 1, src, dst, peer(h, -1))

    def t1(i):
        for h in (0, 1):
            r0, n = PIECES[i][h]
            a, b = half_rows(n)
            D[i, h, 0].wait_recv()
            v = blk(h, -1, r0, a)
            go(i, h, 2, v, v, peer(h, 1))
            D[i, h, 1].wait_recv()
            v = blk(h, 1, r0 + a, b)
            go(i, h, 3, v, v, peer(h, -1))

    def t2(i):
        for h in (0, 1):
            r0, n = PIECES[i][h]
            D[i, h, 2].wait_recv()
            D[i, h, 3].wait_recv()
            v = line(h, 0, r0, n)
            go(i, h, 4, v, v, peer(1 - h, 1))
            go(i, h, 5, v, v, peer(1 - h, -1))
            go(i, h, 6, v, v, sib)

    def t3(i):
        for h in (0, 1):
            r0, n = PIECES[i][h]
            a, b = half_rows(n)
            D[i, h, 4].wait_recv()
            v = line(h, -1, r0, a)
            go(i, h, 7, v, v, peer(1 - h, 1))
            v = line(h, -1, r0, n)
            go(i, h, 8, v, v, sib)
            D[i, h, 5].wait_recv()
            v = line(h, 1, r0 + a, b)
            go(i, h, 9, v, v, peer(1 - h, -1))
            v = line(h, 1, r0, n)
            go(i, h, 10, v, v, sib)

    def t4(i):
        for h in (0, 1):
            r0, n = PIECES[i][h]
            a, b = half_rows(n)
            D[i, h, 7].wait_recv()
            v = line(h, 2, r0, a)
            go(i, h, 11, v, v, sib)
            D[i, h, 9].wait_recv()
            v = line(h, 2, r0 + a, b)
            go(i, h, 12, v, v, sib)

    def t5(i):
        for h in (0, 1):
            for e in (6, 8, 10, 11, 12):
                D[i, h, e].wait_recv()

    def load_block(c, rows):
        return G[c // 8, (c // 2) % 4, c % 2, rows, :]

    def assemble(src0, dst0, count):
        def body(r, _):
            rows = pl.ds(pl.multiple_of(src0 + r * 16, 16), 16)
            out = pl.ds(pl.multiple_of(dst0 + r * 16, 16), 16)
            acc = jnp.zeros((16, 128), F32)
            for c in range(32):
                v = load_block(c, rows).astype(F32)
                acc = acc + v * v
                X[out, c * 128 : (c + 1) * 128] = (v * gain[0:1, c * 128 : (c + 1) * 128]).astype(BF)
            total = jnp.sum(acc, axis=1, keepdims=True)
            inv[out, :] = lax.rsqrt(total * (1.0 / 4096) + 1e-05)
            return 0

        lax.fori_loop(0, count, body, 0)

    def state_rows():
        def body(r, _):
            rows = pl.ds(pl.multiple_of(ROWS + r * 16, 16), 16)
            out = pl.ds(pl.multiple_of(r * 16, 16), 16)
            for c in range(32):
                WsT[out, c * 128 : (c + 1) * 128] = load_block(c, rows)
            return 0

        lax.fori_loop(0, SROWS // 16, body, 0)

    def project(x0, n, row):
        xs = X[x0 : x0 + n, :]
        scale = inv[x0 : x0 + n, :]
        both = jnp.dot(xs, Wgi[...], preferred_element_type=F32) * scale
        if row is not None:
            gate_out[row : row + n, :] = both[:, :256].astype(BF)
        o = 0 if row is None else HALO + row
        inner_out[o : o + n, :] = both[:, 256:].astype(BF)
        proj = lax.dot_general(
            xs, WsT[...], (((1,), (1,)), ((), ())), preferred_element_type=F32
        )
        proj_out[o : o + n, :] = proj * scale

    def compute(i):
        t5(i)
        if i == 0:
            return
        if i == 1:
            state_rows()
            for cp in wcopies:
                cp.wait()
            assemble(ROWS + SROWS, 256, 1)
            project(256, HALO, None)
        q = i - 1 if i == 1 else i - 1
        assemble(q * 256, 0, 16)
        project(0, 256, q * 256)

    t0(0)
    G[y, x, k, pl.ds(ROWS, SROWS), :] = stp[...].astype(F32).T.astype(BF)
    halo.wait_recv()

    @pl.when(z == 0)
    def _():
        G[y, x, k, pl.ds(ROWS + SROWS, HALO), :] = jnp.zeros((HALO, 128), BF)

    for i in range(1, NP):
        t0(i)
    own.wait()
    for t in range(NP + 4):
        if t < NP:
            t1(t)
        if 0 <= t - 1 < NP:
            t2(t - 1)
        if 0 <= t - 2 < NP:
            t3(t - 2)
        if 0 <= t - 3 < NP:
            t4(t - 3)
        if 0 <= t - 4 < NP:
            compute(t - 4)
    halo.wait_send()
    for cp in D.values():
        cp.wait_send()


def vspec():
    return pl.BlockSpec(memory_space=pltpu.VMEM)


def aspec():
    return pl.BlockSpec(memory_space=pl.ANY)


def gather_project(tokens, state_proj, norm_gain, gate_proj, inner_proj):
    return pl.pallas_call(
        gather_kernel,
        name="gather_project",
        out_shape=(
            jax.ShapeDtypeStruct((ROWS, 256), BF),
            jax.ShapeDtypeStruct((ROWS + HALO, 256), BF),
            jax.ShapeDtypeStruct((ROWS + HALO, SROWS), F32),
        ),
        in_specs=[vspec(), vspec(), vspec(), aspec(), aspec()],
        out_specs=(vspec(), vspec(), vspec()),
        scratch_shapes=[
            pltpu.VMEM((4, 4, 2, GROWS, 128), BF),
            pltpu.VMEM((256 + HALO, 4096), BF),
            pltpu.VMEM((SROWS, 4096), BF),
            pltpu.VMEM((4096, 512), BF),
            pltpu.VMEM((256 + HALO, 1), F32),
            pltpu.SemaphoreType.DMA((NP, 2, 13)),
            pltpu.SemaphoreType.DMA((NP, 2, 13)),
            pltpu.SemaphoreType.DMA((2,)),
            pltpu.SemaphoreType.DMA((3,)),
        ],
        compiler_params=pltpu.CompilerParams(
            collective_id=0, has_side_effects=True, vmem_limit_bytes=VLIM
        ),
    )(tokens, state_proj, norm_gain.reshape(1, -1), gate_proj, inner_proj)


NQ = 8


def scatter_kernel(
    gated, gain, tok, outp, out, g, Wo, PP, LS, SA, SB, SC, SD, RA, RB, RC, RD, EO, ER, scale,
    send, recv, gsem, wsem, lsem, esem,
):
    y, x, k = place()

    def peer(axis, d):
        return chan_id(y, x + d, k) if axis == 0 else chan_id(y + d, x, k)

    sib = chan_id(y, x, 1 - k)

    local = []
    for j in range(16):
        col = pl.multiple_of((2 * j + k) * 128, 128)
        cp = pltpu.make_async_copy(
            outp.at[:, pl.ds(col, 128)], Wo.at[pl.ds(0, 256), pl.ds(j * 128, 128)], lsem.at[j]
        )
        cp.start()
        local.append(cp)

    bar = pltpu.get_barrier_semaphore()
    greet = [sib] + [peer(a, d) for a in (0, 1) for d in (1, -1, 2)]
    for d in greet:
        pl.semaphore_signal(bar, inc=1, device_id={"chan": d}, device_id_type=MESH)
    pl.semaphore_wait(bar, 7)

    pend = []
    wrem = []
    for j in range(16):
        col = pl.multiple_of((2 * j + 1 - k) * 128, 128)
        cp = remote(
            outp.at[:, pl.ds(col, 128)], Wo.at[pl.ds(256, 256), pl.ds(j * 128, 128)],
            wsem.at[0, j], wsem.at[1, j], sib,
        )
        cp.start()
        wrem.append(cp)

    grem = []
    for q in range(4):
        rows = pl.ds(q * 256, 256)
        v = gated[rows, :]
        g[0, rows, :] = (v * gain[...]).astype(BF)
        cp = remote(g.at[0, rows], g.at[1, rows], gsem.at[0, q], gsem.at[1, q], sib)
        cp.start()
        grem.append(cp)
        EO[0, :, q * 256 : (q + 1) * 256] = lax.dot_general(
            jnp.ones((8, 256), F32), v * v, (((1,), (1,)), ((), ())),
            preferred_element_type=F32, precision=lax.Precision.HIGHEST,
        )
    e0 = remote(EO.at[0], ER.at[0], esem.at[0, 0], esem.at[1, 0], sib)
    e0.start()
    pend += [e0]

    for cp in local:
        cp.wait()
    for cp in wrem:
        cp.wait_recv()

    def line(qh, h, d):
        if h == 0:
            return PP.at[qh, :, wrap4(x + d)]
        return PP.at[qh, wrap4(y + d)]

    D = {}

    def go(qh, e, src, dst, chan):
        cp = remote(src, dst, send.at[qh, e], recv.at[qh, e], chan)
        cp.start()
        D[qh, e] = cp

    def u0(qh):
        h = qh % 2
        rows = pl.ds(qh * 128, 128)
        both = jnp.concatenate([g[0, rows, :], g[1, rows, :]], axis=1)
        for n in range(4):
            acc = jnp.dot(both, Wo[:, n * 512 : (n + 1) * 512], preferred_element_type=F32)
            for m in range(4):
                PP[qh, n, m] = acc[:, m * 128 : (m + 1) * 128]
        far = line(qh, h, 2)
        SA[qh, 0] = far[:, 0:64, :].astype(BF)
        go(qh, 0, SA.at[qh, 0], RA.at[qh, 0], peer(h, 1))
        SA[qh, 1] = far[:, 64:128, :].astype(BF)
        go(qh, 1, SA.at[qh, 1], RA.at[qh, 1], peer(h, -1))

    def u1(qh):
        h = qh % 2
        D[qh, 0].wait_recv()
        v = line(qh, h, 1)
        SB[qh, 0, :, 0:64] = (v[:, 0:64, :] + RA[qh, 0].astype(F32)).astype(BF)
        SB[qh, 0, :, 64:128] = v[:, 64:128, :].astype(BF)
        go(qh, 2, SB.at[qh, 0], RB.at[qh, 0], peer(h, 1))
        D[qh, 1].wait_recv()
        v = line(qh, h, -1)
        SB[qh, 1, :, 0:64] = v[:, 0:64, :].astype(BF)
        SB[qh, 1, :, 64:128] = (v[:, 64:128, :] + RA[qh, 1].astype(F32)).astype(BF)
        go(qh, 3, SB.at[qh, 1], RB.at[qh, 1], peer(h, -1))

    def u2(qh):
        h = qh % 2
        D[qh, 2].wait_recv()
        D[qh, 3].wait_recv()
        LS[qh] = line(qh, h, 0)[...] + RB[qh, 0].astype(F32) + RB[qh, 1].astype(F32)
        at = y if h == 0 else x
        far = LS.at[qh, wrap4(at + 2)]
        SC[qh, 0] = far[0:64, :].astype(BF)
        go(qh, 4, SC.at[qh, 0], RC.at[qh, 0], peer(1 - h, 1))
        SC[qh, 1] = far[64:128, :].astype(BF)
        go(qh, 5, SC.at[qh, 1], RC.at[qh, 1], peer(1 - h, -1))

    def u3(qh):
        h = qh % 2
        at = y if h == 0 else x
        D[qh, 4].wait_recv()
        v = LS.at[qh, wrap4(at + 1)]
        SD[qh, 0, 0:64] = (v[0:64, :] + RC[qh, 0].astype(F32)).astype(BF)
        SD[qh, 0, 64:128] = v[64:128, :].astype(BF)
        go(qh, 6, SD.at[qh, 0], RD.at[qh, 0], peer(1 - h, 1))
        D[qh, 5].wait_recv()
        v = LS.at[qh, wrap4(at - 1)]
        SD[qh, 1, 0:64] = v[0:64, :].astype(BF)
        SD[qh, 1, 64:128] = (v[64:128, :] + RC[qh, 1].astype(F32)).astype(BF)
        go(qh, 7, SD.at[qh, 1], RD.at[qh, 1], peer(1 - h, -1))

    def u4(qh):
        h = qh % 2
        at = y if h == 0 else x
        D[qh, 6].wait_recv()
        D[qh, 7].wait_recv()
        total = LS[qh, at] + RD[qh, 0].astype(F32) + RD[qh, 1].astype(F32)
        rows = pl.ds(qh * 128, 128)
        out[rows, :] = (tok[rows, :].astype(F32) + total * scale[rows, :]).astype(BF)

    def energy(stage):
        if stage == 0:
            e0.wait_recv()
            EO[1] = EO[0] + ER[0]
        else:
            for d in (1, 2, 3):
                erem[stage - 1][d - 1].wait_recv()
            EO[stage + 1] = EO[stage] + ER[3 * stage - 2] + ER[3 * stage - 1] + ER[3 * stage]
        if stage < 2:
            cps = []
            for d in (1, 2, 3):
                s = 3 * stage + d
                cp = remote(EO.at[stage + 1], ER.at[s], esem.at[0, s], esem.at[1, s], peer(stage, d))
                cp.start()
                cps.append(cp)
            erem.append(cps)
            pend.extend(cps)
        else:
            factor = lax.rsqrt(EO[3] * (1.0 / DI) + 1e-05)
            one = jnp.where(lax.broadcasted_iota(jnp.int32, (8, 128), 0) == 0, 1.0, 0.0).astype(F32)
            scale[...] = lax.dot_general(
                factor, one, (((0,), (0,)), ((), ())),
                preferred_element_type=F32, precision=lax.Precision.HIGHEST,
            )

    erem = []
    for t in range(4 + 4):
        for qh in ((2 * t, 2 * t + 1) if t < 4 else ()):
            if qh % 2 == 0:
                grem[t].wait_recv()
            u0(qh)
        if t < 3:
            energy(t)
        for stage, fn in ((1, u1), (2, u2), (3, u3), (4, u4)):
            if 0 <= t - stage < 4:
                fn(2 * (t - stage))
                fn(2 * (t - stage) + 1)
    for cp in wrem + grem + pend + list(D.values()):
        cp.wait_send()


def project_scatter(gated, gate_gain, tokens, out_proj):
    big = lambda *s: pltpu.VMEM(s, BF)
    return pl.pallas_call(
        scatter_kernel,
        name="project_scatter",
        out_shape=jax.ShapeDtypeStruct((ROWS, 128), BF),
        in_specs=[vspec(), vspec(), vspec(), aspec()],
        out_specs=vspec(),
        scratch_shapes=[
            big(2, ROWS, 256),
            big(512, 2048),
            pltpu.VMEM((NQ, 4, 4, 128, 128), F32),
            pltpu.VMEM((NQ, 4, 128, 128), F32),
            big(NQ, 2, 4, 64, 128),
            big(NQ, 2, 4, 128, 128),
            big(NQ, 2, 64, 128),
            big(NQ, 2, 128, 128),
            big(NQ, 2, 4, 64, 128),
            big(NQ, 2, 4, 128, 128),
            big(NQ, 2, 64, 128),
            big(NQ, 2, 128, 128),
            pltpu.VMEM((4, 8, ROWS), F32),
            pltpu.VMEM((7, 8, ROWS), F32),
            pltpu.VMEM((ROWS, 128), F32),
            pltpu.SemaphoreType.DMA((NQ, 8)),
            pltpu.SemaphoreType.DMA((NQ, 8)),
            pltpu.SemaphoreType.DMA((2, 4)),
            pltpu.SemaphoreType.DMA((2, 16)),
            pltpu.SemaphoreType.DMA((16,)),
            pltpu.SemaphoreType.DMA((2, 7)),
        ],
        compiler_params=pltpu.CompilerParams(
            collective_id=1, has_side_effects=True, vmem_limit_bytes=VLIM
        ),
    )(gated, gate_gain.reshape(1, -1), tokens, out_proj)


def prefix(value, axis, join, neutral):
    count, mine = (lax.axis_size(axis), lax.axis_index(axis))
    pieces = jax.tree.map(lambda part: lax.all_gather(part, axis), value)
    total = jax.tree.map(
        lambda part, zero: jnp.full_like(part, 0) + jnp.asarray(zero, part.dtype), value, neutral
    )

    def turn(position, total):
        longer = join(total, jax.tree.map(lambda part: part[position], pieces))
        return jax.tree.map(lambda new, old: jnp.where(position < mine, new, old), longer, total)

    return lax.fori_loop(0, count - 1, turn, total)


def causal_mix(padded, weights):
    length = ROWS
    padded = padded.astype(F32)
    summed = jnp.zeros((length, padded.shape[1]), F32)
    for offset in range(K):
        first = HALO - (K - 1) + offset
        summed = summed + weights[offset] * padded[first : first + length]
    return jax.nn.silu(summed)


def combine_pair(earlier_part, later_part):
    return (
        earlier_part[0] * later_part[0],
        later_part[0][:, None, None] * earlier_part[1] + later_part[1],
    )


def local(
    tokens, norm_gain, gate_proj, inner_proj, state_proj, conv_inner, conv_state,
    log_rate, rate_bias, skip_gain, gate_gain, out_proj,
):
    gate_raw, inner_ext, proj_ext = gather_project(
        tokens, state_proj, norm_gain, gate_proj, inner_proj
    )
    heads = log_rate.shape[0]
    start_head = lax.axis_index("chan") * heads
    raw_rate = lax.dynamic_slice(proj_ext, (HALO, 2 * N + start_head), (ROWS, heads))
    inner_conv = causal_mix(inner_ext, conv_inner)
    state_conv = causal_mix(proj_ext[:, : 2 * N], conv_state)
    token_rows = tokens.shape[0]
    blocks = token_rows // Q
    step_size = jax.nn.softplus(raw_rate + rate_bias)
    decay_log = -jnp.exp(log_rate) * step_size
    values = inner_conv.reshape(blocks, Q, heads, P_SIZE)
    in_map = state_conv[:, :N].reshape(blocks, Q, N)
    out_map = state_conv[:, N:].reshape(blocks, Q, N)
    step_rows = step_size.reshape(blocks, Q, heads).transpose(0, 2, 1)
    log_rows = decay_log.reshape(blocks, Q, heads).transpose(0, 2, 1)
    lower_mask = (jnp.arange(Q)[:, None] >= jnp.arange(Q)[None, :]).astype(jnp.float32)
    within = jnp.einsum("chs,ts->cht", log_rows, lower_mask)
    log_gaps = within[..., :, None] - within[..., None, :]
    fading = jnp.exp(jnp.where(lower_mask > 0, log_gaps, -jnp.inf))
    scores = jnp.einsum("ctn,csn->cts", out_map, in_map)
    mixing = scores[:, None] * fading * step_rows[:, :, None, :]
    local_out = jnp.einsum("chts,cshp->cthp", mixing, values)
    tail_weight = jnp.exp(within[..., -1:] - within) * step_rows
    scaled = values * tail_weight.transpose(0, 2, 1)[..., None]
    block_end = jnp.einsum("csn,cshp->chnp", in_map, scaled)
    block_log = within[..., -1]
    through = jnp.cumsum(block_log, axis=0)
    before = through - block_log
    earlier = jnp.arange(blocks)[:, None] > jnp.arange(blocks)[None, :]
    passage = jnp.exp(
        jnp.where(earlier[:, :, None], before[:, None, :] - through[None, :, :], -jnp.inf)
    )
    entering = jnp.einsum("cdh,dhnp->chnp", passage, block_end)
    device_end = jnp.einsum("ch,chnp->hnp", jnp.exp(through[-1:] - through), block_end)
    device_fade = jnp.exp(through[-1])
    identity = (jnp.ones_like(device_fade), jnp.zeros_like(device_end))
    carried = prefix((device_fade, device_end), "seq", combine_pair, identity)[1]
    entering = entering + jnp.exp(before)[:, :, None, None] * carried[None]
    carried_out = jnp.einsum("ctn,chnp->cthp", out_map, entering)
    carried_out = carried_out * jnp.exp(within).transpose(0, 2, 1)[..., None]
    skip_wide = jnp.repeat(skip_gain, P_SIZE)
    ssd_out = (local_out + carried_out).reshape(token_rows, heads * P_SIZE) + skip_wide * inner_conv
    gated_out = ssd_out * jax.nn.silu(gate_raw.astype(jnp.float32))
    return project_scatter(gated_out, gate_gain, tokens, out_proj)


def solution(mesh):
    return jax.shard_map(
        local,
        mesh=mesh,
        in_specs=(
            P("seq", "chan"),
            P(),
            P(None, "chan"),
            P(None, "chan"),
            P("chan", None),
            P(None, "chan"),
            P(),
            P("chan"),
            P("chan"),
            P("chan"),
            P("chan"),
            P("chan", None),
        ),
        out_specs=P("seq", "chan"),
        check_vma=False,
    )
```

time: 365 us -> 187 us (0.51)
  waiting for transfers between devices: 184 us -> 18.6 us
  Pallas kernels: 0 us -> 103 us
  blocking collectives: 71.5 us -> 14.3 us
  matrix products: 41.3 us -> 7.19 us
  local copies, waits for them, and re-layouts: 30.5 us -> 20.2 us
  starting transfers between devices: 7.09 us -> 0.01 us
  other arithmetic: 14.3 us -> 8.85 us
    all_gather x3 -> x0, waiting for transfers between devices: 163 us -> none  [the longest x1 65.9 us: local(): gathered = lax.all_gather(tokens, 'chan', axis=1, tiled=True)]
    pallas_call x0 -> x2, Pallas kernels: none -> 103 us  [the longest x1 62.1 us: gather_project(): pl.pallas_call(gather_kernel, name='gather_project', out_shape=(jax.Shape...]
    all_to_all x2 -> x0, blocking collectives: 54.7 us -> none  [the longest x1 40.9 us: local(): lax.all_to_all(out_proj, 'chan', split_axis=1, concat_axis=0, tiled=True)]
    dot_general x4 -> x0, matrix products: 33.4 us -> none  [the longest x1 11.6 us: local(): jnp.dot(lax.all_gather(shaped, 'chan', axis=1, tiled=True), column_rows,...]
    ppermute x2 -> x0, starting transfers between devices: 6.97 us -> none  [from_behind(): lax.ppermute(value, axis, [(source, source + steps) for source in range(l...]
    reduce_sum x2 -> x0, other arithmetic: 5.17 us -> none  [the longest x1 5.07 us: local(): jnp.mean(widened * widened, axis=1, keepdims=True) + 1e-05]
    all_to_all x1 -> x0, local copies, waits for them, and re-layouts: 4.07 us -> none  [local(): lax.all_to_all(out_proj, 'chan', split_axis=1, concat_axis=0, tiled=True)]
  transfers between devices with their start and end apart: 6 -> 1, of which waited for: 5 -> 1; matrix products, arithmetic and copies ran while one was open for 9% -> 1% of each run, Pallas kernels for 0% -> 0%
where the time goes in v1:
time: 187 us; the launch traced here: 186 us
  Pallas kernels  103 us (55%)
  local copies, waits for them, and re-layouts  20.2 us (11%)
  waiting for transfers between devices  18.6 us (10%)
  blocking collectives  14.3 us (8%)
  between operations  13.6 us (7%)
  other arithmetic  8.85 us (5%)
  matrix products  7.19 us (4%)
    pallas_call x1, Pallas kernels, gather_project(): pl.pallas_call(gather_kernel, name='gather_project', out_shape=(jax.Shape...  62.1 us
    pallas_call x1, Pallas kernels, project_scatter(): pl.pallas_call(scatter_kernel, name='project_scatter', out_shape=jax.Shap...  40.6 us
    all_gather x1, waiting for transfers between devices, prefix(): pieces = jax.tree.map(lambda part: lax.all_gather(part, axis), value)  18.5 us
    all_gather x1, blocking collectives, prefix(): pieces = jax.tree.map(lambda part: lax.all_gather(part, axis), value)  14.3 us
    dynamic_slice x14, local copies, waits for them, and re-layouts, turn(): longer = join(total, jax.tree.map(lambda part: part[position], pieces))  7.32 us
    reshape x2, local copies, waits for them, and re-layouts, local(): (local_out + carried_out).reshape(token_rows, heads * P_SIZE)  3.95 us
  transfers between devices with their start and end apart: 1, of which 1 were waited for; matrix products, arithmetic and copies ran while one was open for 1% of the time, Pallas kernels for 0%

profile of v1, /device:TPU:2, one launch (start us, length us, event | category | flops | bytes accessed | tf_op | source)
XLA Modules:
  0.0 185.8 jit_solution(10614839963948005495)
XLA Ops:
  6.5 0.7 exponential_negate_fusion
  7.2 62.1 %gather_project.1 = (bf16[1024,256]{1,0:T(8,128)(2,1)}, bf16[1040,256]{1,0:T(8,128)(2,1)}, f32[1040,384]{1,0:T(8,128)}) custom-call(bf16[1024,128]{1,0:T(8,128)(2,1)} %tok.3, bf16[128,384]{1,0:T(8,128)(2,1)} %stp.1, f32[1,4096]{1,0:T(1,128)} %bitcast.88, bf16[4096,256]{1,0:T(8,128)(2,1)} %gate_hbm.1, bf16[4096,256]{1,0:T(8,128)(2,1)} %inner_hbm.1), custom_call_target="tpu_custom_call" | custom-call | tf_op jit(solution)/shard_map/gather_project/pallas_call | solution.py:262
  69.3 0.0 copy-start.5
  69.3 0.0 copy-start.4
  69.3 0.0 copy-done.7
  69.3 1.5 broadcast_multiply_fusion.1
  70.8 0.1 copy.54
  71.0 0.2 fusion.33
  71.1 0.2 slice_reduce_fusion
  71.3 0.2 copy.57
  71.5 0.1 bitcast_multiply_fusion.1
  71.6 0.0 copy-done.5
  71.7 0.1 convert_element_type.9
  71.8 1.6 divide_multiply_fusion.1
  73.4 2.7 %copy.52 = f32[1024,256]{0,1:T(8,128)} copy(f32[1024,256]{1,0:T(8,128)} %divide_multiply_fusion.1) | data formatting | bytes 2097152 | tf_op jit(solution)/shard_map/jit(silu)/mul | solution.py:523
  76.0 2.7 %reshape.64 = f32[4,256,4,64]{1,0,3,2:T(4,128)} reshape(f32[1024,256]{0,1:T(8,128)} %copy.52) | data formatting | bytes 2097152 | tf_op jit(solution)/shard_map/reshape | solution.py:549
  78.8 0.0 copy-done
  78.8 0.0 copy-start.1
  78.8 0.6 divide_multiply_fusion
  79.4 0.0 copy-start.8
  79.5 0.5 copy-done.1
  80.0 0.2 broadcast_multiply_fusion
  80.2 1.6 fusion.30
  81.8 0.0 all-gather.4.cloned.1.call-update
  81.9 0.1 copy.61
  82.0 0.1 copy.60
  82.1 0.1 copy.63
  82.1 0.2 copy.55
  82.3 0.1 broadcast_in_dim.29
  82.4 0.1 mul.228
  82.5 14.3 %all-gather.1 = f32[8,1,4]{2,1,0:T(1,128)S(1)} all-gather(f32[1,1,4]{2,1,0:T(1,128)S(1)} %get-tuple-element.170), channel_id=1, replica_groups=mesh['seq'=8,'chan'=32] {'seq'}, dimensions={0}, use_global_device_ids=true | all-gather | bytes 144 | tf_op jit(solution)/shard_map/all_gather | solution.py:504
  96.9 1.3 fusion.50
  98.1 18.5 %all-gather.4.cloned.1.call-done = f32[32,128,64]{1,2,0:T(8,128)} async-done(((f32[4,128,64]{1,2,0:T(8,128)}), f32[32,128,64]{1,2,0:T(8,128)}) %all-gather.4.cloned.1.call-update) | async-done | bytes 1048592 | tf_op jit(solution)/shard_map/all_gather | solution.py:504
  116.7 8.4 %while.14 = (s32[]{:T(128)}, f32[4,128,64]{2,1,0:T(8,128)S(1)}, s32[]{:T(128)}, f32[8,4]{1,0:T(8,128)S(1)}, f32[8,4,128,64]{2,3,1,0:T(8,128)}, /*index=5*/s32[]{:T(128)}, s32[]{:T(128)}) while((s32[]{:T(128)}, f32[4,128,64]{2,1,0:T(8,128)S(1)}, s32[]{:T(128)}, f32[8,4]{1,0:T(8,128)S(1)}, f32[8,4,128,64]{2,3,1,0:T(8,128)}, ...), condition=%wide.region_2.3_spmd.clone, body=%wide.region_1.2_spmd.clone.sunk | while | flops 131076 | bytes 917657 | solution.py:513
  116.7 0.9 constant_dynamic-slice_fusion.2
  117.6 0.1 copy.91
  117.8 0.1 fusion.58
  117.9 0.9 constant_dynamic-slice_fusion.2
  118.8 0.1 copy.91
  119.0 0.1 fusion.58
  119.1 0.9 constant_dynamic-slice_fusion.2
  120.0 0.1 copy.91
  120.2 0.1 fusion.58
  120.3 0.9 constant_dynamic-slice_fusion.2
  121.2 0.1 copy.91
  121.4 0.1 fusion.58
  121.5 0.9 constant_dynamic-slice_fusion.2
  122.4 0.1 copy.91
  122.6 0.1 fusion.58
  122.7 0.9 constant_dynamic-slice_fusion.2
  123.6 0.1 copy.91
  123.8 0.1 fusion.58
  123.9 0.9 constant_dynamic-slice_fusion.2
  124.8 0.1 copy.91
  125.0 0.1 fusion.58
  125.1 0.1 copy.67
  125.2 1.4 fusion.19
  126.7 0.3 fusion.51
  127.0 2.4 %fusion.16 = f32[4,256,4,64]{1,3,2,0:T(8,128)} fusion(f32[4,4,256]{2,1,0:T(4,128)S(1)} %copy.55, f32[4,4,256]{2,1,0:T(4,128)S(1)} %fusion.33, f32[4,256,256]{2,1,0:T(8,128)S(1)} %copy-done.3, pred[256,256]{1,0:T(8,128)(4,1)S(1)} %convert_compare_fusion, f32[4,256,4,64]{1,0,3,2:T(4,128)S(1)} %copy-done.2, f32[4,256,4,64]{1,3,2,0:T(8,128)S(1)} %bitcast.82, ...), kind=kOutput, calls=%fused_computation.18 | convolution fusion | flops 138936320 | bytes 4308992 | tf_op jit(solution)/shard_map/chts,cshp->cthp/dot_general | solution.py:560
  129.4 1.8 copy.79
  131.2 2.1 %reshape.81 = f32[1024,256]{1,0:T(8,128)} reshape(f32[4,256,4,64]{3,2,1,0:T(4,128)S(1)} %copy.79) | data formatting | bytes 2097152 | tf_op jit(solution)/shard_map/reshape | solution.py:580
  133.4 3.3 %fusion.23.gated = f32[1024,256]{1,0:T(8,128)} fusion(bf16[1024,256]{1,0:T(8,128)(2,1)} %get-tuple-element.105, f32[1024,256]{1,0:T(8,128)} %reshape.81, f32[256]{0:T(256)S(1)} %mul.228, f32[1040,256]{1,0:T(8,128)S(1)} %convert_element_type.9, f32[256]{0:T(256)S(1)} %bitcast.94, f32[256]{0:T(256)S(1)} %bitcast.96, f32[256]{0:T(256)S(1)} %bitcast.92, ...), kind=kLoop, calls=%fused_computation.26 | loop fusion | flops 4980736 | bytes 6820864 | tf_op jit(solution)/shard_map/mul | solution.py:581
  136.6 40.6 %project_scatter.1 = bf16[1024,128]{1,0:T(8,128)(2,1)} custom-call(f32[1024,256]{1,0:T(8,128)} %fusion.23.gated, f32[1,256]{1,0:T(1,128)} %bitcast.102, bf16[1024,128]{1,0:T(8,128)(2,1)} %tok.3, bf16[256,4096]{1,0:T(8,128)(2,1)} %outp.1), custom_call_target="tpu_custom_call" | custom-call | tf_op jit(solution)/shard_map/project_scatter/pallas_call | solution.py:467
  177.3 1.7 copy.99
  (30 shorter events, 0.3 us)
Async XLA Ops:
  6.5 110.1 %all-gather.4.cloned.1.call-start = ((), (), s32[]{:S(2)}) async-start(), calls=%async_computation | async-start | bytes 1179648 | tf_op jit(solution)/shard_map/all_gather | solution.py:504
  7.2 62.1 %copy-start.7 = (f32[4]{0:T(128)S(1)}, f32[4]{0:T(128)}, u32[]{:S(2)}) copy-start(f32[4]{0:T(128)} %param.22) | copy-start | bytes 52
  69.3 2.4 %copy-start.5 = (f32[4,256]{1,0:T(4,128)S(1)}, f32[4,256]{1,0:T(4,128)}, u32[]{:S(2)}) copy-start(f32[4,256]{1,0:T(4,128)} %param.19) | copy-start | bytes 12292
  69.3 2.4 %copy-start.4 = (bf16[1040,256]{1,0:T(8,128)(2,1)S(1)}, bf16[1040,256]{1,0:T(8,128)(2,1)}, u32[]{:S(2)}) copy-start(bf16[1040,256]{1,0:T(8,128)(2,1)} %get-tuple-element.102) | copy-start | bytes 1597444
  73.4 5.4 %copy-start.6 = (f32[4,256]{1,0:T(4,128)S(1)}, f32[4,256]{1,0:T(4,128)}, u32[]{:S(2)}) copy-start(f32[4,256]{1,0:T(4,128)} %param.20) | copy-start | bytes 12292
  73.4 5.4 %copy-start = (f32[1040,384]{1,0:T(8,128)S(1)}, f32[1040,384]{1,0:T(8,128)}, u32[]{:S(2)}) copy-start(f32[1040,384]{1,0:T(8,128)} %get-tuple-element.103) | copy-start | bytes 4792324
  78.8 1.2 copy-start.1
  79.4 2.9 %copy-start.8 = (f32[4]{0:T(128)S(1)}, f32[4]{0:T(128)}, u32[]{:S(2)}) copy-start(f32[4]{0:T(128)} %param.23) | copy-start | bytes 52
  125.1 1.9 %copy-start.2 = (f32[4,256,4,64]{1,0,3,2:T(4,128)S(1)}, f32[4,256,4,64]{1,0,3,2:T(4,128)}, u32[]{:S(2)}) copy-start(f32[4,256,4,64]{1,0,3,2:T(4,128)} %reshape.64) | copy-start | bytes 3145732
  125.2 1.8 copy-start.3
Sparse Core Ops, SparseCore 0:
  82.0 34.6 all-gather.3

commit v2 on v1

--- a/solution.py
+++ b/solution.py
@@ -252,6 +252,10 @@
 
 def vspec():
     return pl.BlockSpec(memory_space=pltpu.VMEM)
+
+
+def sspec():
+    return pl.BlockSpec(memory_space=pltpu.SMEM)
 
 
 def aspec():
@@ -289,11 +293,14 @@
 NQ = 8
 
 
-def scatter_kernel(
-    gated, gain, tok, outp, out, g, Wo, PP, LS, SA, SB, SC, SD, RA, RB, RC, RD, EO, ER, scale,
-    send, recv, gsem, wsem, lsem, esem,
+def ssd_scatter_kernel(
+    inner, proj, gate, cw, cs, log_rate, rate_bias, skip, gain, tok, outp, out,
+    g, Wo, PP, LS, SA, SB, SC, SD, RA, RB, RC, RD, EO, ER, scale,
+    XC, BC, WI, DT, BE, SE, Y, ZB,
+    send, recv, gsem, wsem, lsem, esem, zsem,
 ):
     y, x, k = place()
+    z = lax.axis_index("seq")
 
     def peer(axis, d):
         return chan_id(y, x + d, k) if axis == 0 else chan_id(y + d, x, k)
@@ -313,7 +320,9 @@
     greet = [sib] + [peer(a, d) for a in (0, 1) for d in (1, -1, 2)]
     for d in greet:
         pl.semaphore_signal(bar, inc=1, device_id={"chan": d}, device_id_type=MESH)
-    pl.semaphore_wait(bar, 7)
+    for dz in (1, 7):
+        pl.semaphore_signal(bar, inc=1, device_id={"seq": lax.rem(z + dz, 8)}, device_id_type=MESH)
+    pl.semaphore_wait(bar, 9)
 
     pend = []
     wrem = []
@@ -326,10 +335,157 @@
         cp.start()
         wrem.append(cp)
 
+    lane = lax.broadcasted_iota(jnp.int32, (1, 128), 1)
+
+    def lanes(ref):
+        row = jnp.zeros((1, 128), F32)
+        for h in range(4):
+            row = jnp.where(lane == h, ref[h], row)
+        return row
+
+    def wide(v):
+        return jnp.concatenate(
+            [jnp.where(lane < 64, v[:, 0:1], v[:, 1:2]), jnp.where(lane < 64, v[:, 2:3], v[:, 3:4])],
+            axis=1,
+        )
+
+    bias_row = lanes(rate_bias)
+    rate_row = jnp.where(lane < 4, -jnp.exp(lanes(log_rate)), 0.0)
+    skip_row = wide(lanes(skip))
+    shift = lax.rem(128 - 4 * lax.axis_index("chan"), 128)
+    lower = lax.broadcasted_iota(jnp.int32, (Q, Q), 0) >= lax.broadcasted_iota(jnp.int32, (Q, Q), 1)
+
+    def silu(v):
+        return v / (1.0 + jnp.exp(-v))
+
+    def mix(v, w):
+        total = w[0:1, :] * v[13 : 13 + Q]
+        for j in range(1, K):
+            total = total + w[j : j + 1, :] * v[13 + j : 13 + j + Q]
+        return silu(total)
+
+    def softplus(v):
+        u = jnp.exp(-jnp.abs(v))
+        small = u * (1.0 + u * (-0.5 + u * (1.0 / 3 + u * (-0.25 + u * 0.2))))
+        return jnp.maximum(v, 0.0) + jnp.where(u < 0.03, small, jnp.log(1.0 + u))
+
+    def split3(v):
+        hi = v.astype(BF)
+        rest = v - hi.astype(F32)
+        mid = rest.astype(BF)
+        return hi, mid, (rest - mid.astype(F32)).astype(BF)
+
+    SE[0] = jnp.zeros((N, 256), F32)
+    BE[0] = jnp.zeros((8, 128), F32)
+
+    def states(b, _):
+        r0 = pl.multiple_of(b * Q, Q)
+        rows = pl.ds(r0, Q)
+        xs = mix(inner[pl.ds(r0, Q + HALO), :].astype(F32), cw[...])
+        XC[rows, :] = xs
+        maps = mix(proj[pl.ds(r0, Q + HALO), 0:256], cs[...]).astype(BF)
+        BC[rows, :] = maps
+        rate = pltpu.roll(proj[pl.ds(pl.multiple_of(r0 + HALO, 16), Q), 256:384], shift, 1)
+        step = softplus(rate + bias_row)
+        decay = rate_row * step
+        tri = lower.astype(F32).astype(BF)
+        within = jnp.zeros((Q, 128), F32)
+        for part in split3(decay):
+            within = within + jnp.dot(tri, part, preferred_element_type=F32)
+        DT[rows, :] = step
+        WI[rows, :] = within
+        last = within[Q - 1 : Q, :]
+        BE[b + 1] = BE[b] + last
+        weighted = (xs * wide(jnp.exp(last - within) * step)).astype(BF)
+        fresh = lax.dot_general(
+            maps[:, 0:N], weighted, (((0,), (0,)), ((), ())), preferred_element_type=F32
+        )
+        SE[b + 1] = wide(jnp.exp(last)) * SE[b] + fresh
+        return 0
+
+    lax.fori_loop(0, 4, states, 0)
+
+    sub = lax.broadcasted_iota(jnp.int32, (16, 128), 0)
+    total_row = wide(BE[4][0:1, :])
+    for j in range(2):
+        cols = slice(j * 128, (j + 1) * 128)
+        ZB[z, j, 0:N, :] = SE[4, :, cols].astype(BF)
+        hi, mid, lo = [p.astype(F32) for p in split3(total_row[:, cols])]
+        ZB[z, j, N : N + 16, :] = jnp.where(
+            sub == 0, hi, jnp.where(sub == 1, mid, jnp.where(sub == 2, lo, 0.0))
+        ).astype(BF)
+
+    ZD = {}
+
+    def zgo(way, s, j):
+        at = lax.rem(z - s + 9, 8) if way == 0 else lax.rem(z + s - 1, 8)
+        to = lax.rem(z + 1, 8) if way == 0 else lax.rem(z + 7, 8)
+        cp = pltpu.make_async_remote_copy(
+            src_ref=ZB.at[at, j], dst_ref=ZB.at[at, j],
+            send_sem=zsem.at[0, way, s - 1, j], recv_sem=zsem.at[1, way, s - 1, j],
+            device_id={"seq": to}, device_id_type=MESH,
+        )
+        cp.start()
+        ZD[way, s, j] = cp
+        pend.append(cp)
+
+    def zstep(s):
+        for j in range(2):
+            for way in range(2):
+                if s > 1:
+                    ZD[way, s - 1, j].wait_recv()
+                if s < 4 or j == way:
+                    zgo(way, s, j)
+
+    def inside(b):
+        rows = pl.ds(b * Q, Q)
+        xs = XC[rows, :]
+        xb = xs.astype(BF)
+        im, om = BC[rows, 0:N], BC[rows, N:]
+        within, step = WI[rows, :], DT[rows, :]
+        scores = lax.dot_general(om, im, (((1,), (1,)), ((), ())), preferred_element_type=F32)
+        within_t, step_t = within.T, step.T
+        parts = []
+        for h in range(4):
+            gap = within[:, h : h + 1] - within_t[h : h + 1, :]
+            fading = jnp.exp(jnp.where(lower, gap, -1e30))
+            mixing = (scores * fading * step_t[h : h + 1, :]).astype(BF)
+            pair = h // 2
+            parts.append(
+                jnp.dot(mixing, xb[:, pair * 128 : (pair + 1) * 128], preferred_element_type=F32)
+            )
+        near = jnp.concatenate(
+            [jnp.where(lane < 64, parts[0], parts[1]), jnp.where(lane < 64, parts[2], parts[3])],
+            axis=1,
+        )
+        far = jnp.dot(om, SE[b].astype(BF), preferred_element_type=F32)
+        Y[rows, :] = near + far * wide(jnp.exp(within)) + skip_row * xs
+
+    zstep(1)
+    for b in range(4):
+        inside(b)
+        if b < 3:
+            zstep(b + 2)
+    ZD[0, 4, 0].wait_recv()
+    ZD[1, 4, 1].wait_recv()
+
+    halves = []
+    for j in range(2):
+        state = jnp.zeros((N, 128), F32)
+        for s in range(7):
+            tail = ZB[s, j, N : N + 16, :].astype(F32)
+            fade = jnp.exp(tail[0:1] + tail[1:2] + tail[2:3])
+            longer = state * fade + ZB[s, j, 0:N, :].astype(F32)
+            state = jnp.where(s < z, longer, state)
+        halves.append(state)
+    carried = jnp.concatenate(halves, axis=1).astype(BF)
+
     grem = []
     for q in range(4):
         rows = pl.ds(q * 256, 256)
-        v = gated[rows, :]
+        far = jnp.dot(BC[rows, N:], carried, preferred_element_type=F32)
+        v = Y[rows, :] + far * wide(jnp.exp(BE[q][0:1, :] + WI[rows, :]))
+        v = v * silu(gate[rows, :].astype(F32))
         g[0, rows, :] = (v * gain[...]).astype(BF)
         cp = remote(g.at[0, rows], g.at[1, rows], gsem.at[0, q], gsem.at[1, q], sib)
         cp.start()
@@ -462,13 +618,13 @@
         cp.wait_send()
 
 
-def project_scatter(gated, gate_gain, tokens, out_proj):
+def ssd_scatter(inner, proj, gate, conv_inner, conv_state, log_rate, rate_bias, skip_gain, gate_gain, tokens, out_proj):
     big = lambda *s: pltpu.VMEM(s, BF)
     return pl.pallas_call(
-        scatter_kernel,
-        name="project_scatter",
+        ssd_scatter_kernel,
+        name="ssd_scatter",
         out_shape=jax.ShapeDtypeStruct((ROWS, 128), BF),
-        in_specs=[vspec(), vspec(), vspec(), aspec()],
+        in_specs=[vspec()] * 5 + [sspec()] * 3 + [vspec(), vspec(), aspec()],
         out_specs=vspec(),
         scratch_shapes=[
             big(2, ROWS, 256),
@@ -486,47 +642,28 @@
             pltpu.VMEM((4, 8, ROWS), F32),
             pltpu.VMEM((7, 8, ROWS), F32),
             pltpu.VMEM((ROWS, 128), F32),
+            pltpu.VMEM((ROWS, 256), F32),
+            big(ROWS, 256),
+            pltpu.VMEM((ROWS, 128), F32),
+            pltpu.VMEM((ROWS, 128), F32),
+            pltpu.VMEM((5, 8, 128), F32),
+            pltpu.VMEM((5, N, 256), F32),
+            pltpu.VMEM((ROWS, 256), F32),
+            big(8, 2, N + 16, 128),
             pltpu.SemaphoreType.DMA((NQ, 8)),
             pltpu.SemaphoreType.DMA((NQ, 8)),
             pltpu.SemaphoreType.DMA((2, 4)),
             pltpu.SemaphoreType.DMA((2, 16)),
             pltpu.SemaphoreType.DMA((16,)),
             pltpu.SemaphoreType.DMA((2, 7)),
+            pltpu.SemaphoreType.DMA((2, 2, 4, 2)),
         ],
         compiler_params=pltpu.CompilerParams(
             collective_id=1, has_side_effects=True, vmem_limit_bytes=VLIM
         ),
-    )(gated, gate_gain.reshape(1, -1), tokens, out_proj)
-
-
-def prefix(value, axis, join, neutral):
-    count, mine = (lax.axis_size(axis), lax.axis_index(axis))
-    pieces = jax.tree.map(lambda part: lax.all_gather(part, axis), value)
-    total = jax.tree.map(
-        lambda part, zero: jnp.full_like(part, 0) + jnp.asarray(zero, part.dtype), value, neutral
-    )
-
-    def turn(position, total):
-        longer = join(total, jax.tree.map(lambda part: part[position], pieces))
-        return jax.tree.map(lambda new, old: jnp.where(position < mine, new, old), longer, total)
-
-    return lax.fori_loop(0, count - 1, turn, total)
-
-
-def causal_mix(padded, weights):
-    length = ROWS
-    padded = padded.astype(F32)
-    summed = jnp.zeros((length, padded.shape[1]), F32)
-    for offset in range(K):
-        first = HALO - (K - 1) + offset
-        summed = summed + weights[offset] * padded[first : first + length]
-    return jax.nn.silu(summed)
-
-
-def combine_pair(earlier_part, later_part):
-    return (
-        earlier_part[0] * later_part[0],
-        later_part[0][:, None, None] * earlier_part[1] + later_part[1],
+    )(
+        inner, proj, gate, conv_inner, conv_state, log_rate, rate_bias, skip_gain,
+        gate_gain.reshape(1, -1), tokens, out_proj,
     )
 
 
@@ -537,49 +674,10 @@
     gate_raw, inner_ext, proj_ext = gather_project(
         tokens, state_proj, norm_gain, gate_proj, inner_proj
     )
-    heads = log_rate.shape[0]
-    start_head = lax.axis_index("chan") * heads
-    raw_rate = lax.dynamic_slice(proj_ext, (HALO, 2 * N + start_head), (ROWS, heads))
-    inner_conv = causal_mix(inner_ext, conv_inner)
-    state_conv = causal_mix(proj_ext[:, : 2 * N], conv_state)
-    token_rows = tokens.shape[0]
-    blocks = token_rows // Q
-    step_size = jax.nn.softplus(raw_rate + rate_bias)
-    decay_log = -jnp.exp(log_rate) * step_size
-    values = inner_conv.reshape(blocks, Q, heads, P_SIZE)
-    in_map = state_conv[:, :N].reshape(blocks, Q, N)
-    out_map = state_conv[:, N:].reshape(blocks, Q, N)
-    step_rows = step_size.reshape(blocks, Q, heads).transpose(0, 2, 1)
-    log_rows = decay_log.reshape(blocks, Q, heads).transpose(0, 2, 1)
-    lower_mask = (jnp.arange(Q)[:, None] >= jnp.arange(Q)[None, :]).astype(jnp.float32)
-    within = jnp.einsum("chs,ts->cht", log_rows, lower_mask)
-    log_gaps = within[..., :, None] - within[..., None, :]
-    fading = jnp.exp(jnp.where(lower_mask > 0, log_gaps, -jnp.inf))
-    scores = jnp.einsum("ctn,csn->cts", out_map, in_map)
-    mixing = scores[:, None] * fading * step_rows[:, :, None, :]
-    local_out = jnp.einsum("chts,cshp->cthp", mixing, values)
-    tail_weight = jnp.exp(within[..., -1:] - within) * step_rows
-    scaled = values * tail_weight.transpose(0, 2, 1)[..., None]
-    block_end = jnp.einsum("csn,cshp->chnp", in_map, scaled)
-    block_log = within[..., -1]
-    through = jnp.cumsum(block_log, axis=0)
-    before = through - block_log
-    earlier = jnp.arange(blocks)[:, None] > jnp.arange(blocks)[None, :]
-    passage = jnp.exp(
-        jnp.where(earlier[:, :, None], before[:, None, :] - through[None, :, :], -jnp.inf)
+    return ssd_scatter(
+        inner_ext, proj_ext, gate_raw, conv_inner, conv_state, log_rate, rate_bias, skip_gain,
+        gate_gain, tokens, out_proj,
     )
-    entering = jnp.einsum("cdh,dhnp->chnp", passage, block_end)
-    device_end = jnp.einsum("ch,chnp->hnp", jnp.exp(through[-1:] - through), block_end)
-    device_fade = jnp.exp(through[-1])
-    identity = (jnp.ones_like(device_fade), jnp.zeros_like(device_end))
-    carried = prefix((device_fade, device_end), "seq", combine_pair, identity)[1]
-    entering = entering + jnp.exp(before)[:, :, None, None] * carried[None]
-    carried_out = jnp.einsum("ctn,chnp->cthp", out_map, entering)
-    carried_out = carried_out * jnp.exp(within).transpose(0, 2, 1)[..., None]
-    skip_wide = jnp.repeat(skip_gain, P_SIZE)
-    ssd_out = (local_out + carried_out).reshape(token_rows, heads * P_SIZE) + skip_wide * inner_conv
-    gated_out = ssd_out * jax.nn.silu(gate_raw.astype(jnp.float32))
-    return project_scatter(gated_out, gate_gain, tokens, out_proj)
 
 
 def solution(mesh):

time: 187 us -> 122 us (0.65)
  waiting for transfers between devices: 18.6 us -> 0 us
  local copies, waits for them, and re-layouts: 20.2 us -> 1.67 us
  Pallas kernels: 103 us -> 120 us
  blocking collectives: 14.3 us -> 0 us
  between operations: 13.6 us -> 0.02 us
  other arithmetic: 8.85 us -> 0 us
  matrix products: 7.19 us -> 0 us
    all_gather x1 -> x0, waiting for transfers between devices: 18.5 us -> none  [prefix(): pieces = jax.tree.map(lambda part: lax.all_gather(part, axis), value)]
    pallas_call x1, Pallas kernels: 40.6 us -> 58.5 us  [ssd_scatter(): pl.pallas_call(ssd_scatter_kernel, name='ssd_scatter', out_shape=jax.Shap...]
    all_gather x1 -> x0, blocking collectives: 14.3 us -> none  [prefix(): pieces = jax.tree.map(lambda part: lax.all_gather(part, axis), value)]
    mul x6 -> x0, other arithmetic: 7.32 us -> none  [the longest x1 3.29 us: local(): gated_out = ssd_out * jax.nn.silu(gate_raw.astype(jnp.float32))]
    dynamic_slice x14 -> x0, local copies, waits for them, and re-layouts: 7.32 us -> none  [turn(): longer = join(total, jax.tree.map(lambda part: part[position], pieces))]
    reshape x5 -> x0, local copies, waits for them, and re-layouts: 6.98 us -> none  [the longest x2 3.95 us: local(): (local_out + carried_out).reshape(token_rows, heads * P_SIZE)]
    dot_general x5 -> x0, matrix products: 6.9 us -> none  [the longest x1 2.36 us: local(): local_out = jnp.einsum('chts,cshp->cthp', mixing, values)]
    mul x10 -> x0, local copies, waits for them, and re-layouts: 2.81 us -> none  [the longest x1 2.65 us: causal_mix(): return jax.nn.silu(summed)]
  transfers between devices with their start and end apart: 1 -> 0, of which waited for: 1 -> 0; matrix products, arithmetic and copies ran while one was open for 1% -> 0% of each run, Pallas kernels for 0% -> 0%
where the time goes in v2:
time: 122 us
  Pallas kernels  120 us (98%)
  local copies, waits for them, and re-layouts  1.67 us (1%)
    pallas_call x1, Pallas kernels, gather_project(): pl.pallas_call(gather_kernel, name='gather_project', out_shape=(jax.Shape...  62 us
    pallas_call x1, Pallas kernels, ssd_scatter(): pl.pallas_call(ssd_scatter_kernel, name='ssd_scatter', out_shape=jax.Shap...  58.5 us

profile of v2, /device:TPU:2, one launch (start us, length us, event | category | flops | bytes accessed | tf_op | source)
XLA Modules:
  0.0 122.1 jit_solution(9298059418578947265)
XLA Ops:
  0.0 62.0 %gather_project.1 = (bf16[1024,256]{1,0:T(8,128)(2,1)}, bf16[1040,256]{1,0:T(8,128)(2,1)}, f32[1040,384]{1,0:T(8,128)}) custom-call(bf16[1024,128]{1,0:T(8,128)(2,1)} %tok.3, bf16[128,384]{1,0:T(8,128)(2,1)} %stp.1, f32[1,4096]{1,0:T(1,128)} %bitcast.2, bf16[4096,256]{1,0:T(8,128)(2,1)} %gate_hbm.1, bf16[4096,256]{1,0:T(8,128)(2,1)} %inner_hbm.1), custom_call_target="tpu_custom_call" | custom-call | tf_op jit(solution)/shard_map/gather_project/pallas_call | solution.py:266
  62.0 58.5 %ssd_scatter.1 = bf16[1024,128]{1,0:T(8,128)(2,1)} custom-call(bf16[1040,256]{1,0:T(8,128)(2,1)} %get-tuple-element.8.inner, f32[1040,384]{1,0:T(8,128)} %get-tuple-element.9.proj, bf16[1024,256]{1,0:T(8,128)(2,1)} %get-tuple-element.10.gate, f32[4,256]{1,0:T(4,128)} %cw.1, f32[4,256]{1,0:T(4,128)} %cs.1, f32[4]{0:T(128)} %log_rate.1, f32[4]{0:T(128)} %rate_bias.1, ...), custom_call_target="tpu_custom_call" | custom-call | tf_op jit(solution)/shard_map/ssd_scatter/pallas_call | solution.py:623
  120.4 1.7 %copy.14 = bf16[1024,128]{1,0:T(8,128)(2,1)} copy(bf16[1024,128]{1,0:T(8,128)(2,1)} %ssd_scatter.1) | data formatting | bytes 524288

commit v3 on v1

v3 whole, which is shorter than its diff:
```python
import functools

import jax
import jax.numpy as jnp
from jax import lax
from jax.experimental import pallas as pl
from jax.experimental.pallas import tpu as pltpu
from jax.sharding import PartitionSpec as P

P_SIZE = 64
N = 128
K = 4
Q = 256
DI = 8192
F32 = jnp.float32
BF = jnp.bfloat16
MESH = pl.DeviceIdType.MESH
HALO = 16
VLIM = 62 * 1024 * 1024


def place():
    c = lax.axis_index("chan")
    k = lax.rem(c, 2)
    chip = c // 2
    return chip // 4, lax.rem(chip, 4), k


def wrap4(v):
    return lax.rem(v + 4, 4)


def chan_id(y, x, k):
    return (wrap4(y) * 4 + wrap4(x)) * 2 + k


def remote(src, dst, send, recv, chan):
    return pltpu.make_async_remote_copy(
        src_ref=src, dst_ref=dst, send_sem=send, recv_sem=recv,
        device_id={"chan": chan}, device_id_type=MESH,
    )


ROWS = 1024
SROWS = 384
SBASE = HALO + ROWS
GROWS = SBASE + SROWS
NQ = 8
PIECES = [((SBASE, 192), (SBASE + 192, 192)), ((0, 144), (144, 128))] + [
    ((HALO + q * 256, 128), (HALO + q * 256 + 128, 128)) for q in (1, 2, 3)
]
NP = len(PIECES)


def half_rows(n):
    a = (n // 2 + 15) // 16 * 16
    return a, n - a


def layer_kernel(
    tok, stp, gain_in, gate_hbm, inner_hbm, cw, cs, log_rate, rate_bias, skip, gain, outp, out,
    G, X, W, SQ, inv, IN, PJ, GT,
    g, Wo, PP, LS, SA, SB, SC, SD, RA, RB, RC, RD, EO, ER, scale,
    XC, BC, WI, DT, BE, SE, Y, EG, ZB,
    gsend, grecv, hsem, osem,
    send, recv, gsem, wsem, lsem, esem, zsem,
):
    y, x, k = place()
    z = lax.axis_index("seq")

    def peer(axis, d):
        return chan_id(y, x + d, k) if axis == 0 else chan_id(y + d, x, k)

    sib = chan_id(y, x, 1 - k)

    own = [pltpu.make_async_copy(tok, G.at[y, x, k, pl.ds(HALO, ROWS)], osem.at[0])]
    for j in range(3):
        own.append(
            pltpu.make_async_copy(
                stp.at[:, pl.ds(j * 128, 128)], G.at[y, x, k, pl.ds(SBASE + j * 128, 128)], osem.at[1 + j]
            )
        )
    wcopies = [
        pltpu.make_async_copy(gate_hbm, W.at[:, 0:256], osem.at[4]),
        pltpu.make_async_copy(inner_hbm, W.at[:, 256:512], osem.at[5]),
    ]
    for cp in own + wcopies:
        cp.start()

    bar = pltpu.get_barrier_semaphore()
    for d in [sib] + [peer(a, d) for a in (0, 1) for d in (1, -1, 2)]:
        pl.semaphore_signal(bar, inc=1, device_id={"chan": d}, device_id_type=MESH)
    for dz in (1, 7):
        pl.semaphore_signal(bar, inc=1, device_id={"seq": lax.rem(z + dz, 8)}, device_id_type=MESH)
    pl.semaphore_wait(bar, 9)

    halo = pltpu.make_async_remote_copy(
        src_ref=tok.at[pl.ds(ROWS - HALO, HALO)],
        dst_ref=G.at[y, x, k, pl.ds(0, HALO)],
        send_sem=hsem.at[0], recv_sem=hsem.at[1],
        device_id={"seq": lax.rem(z + 1, 8)}, device_id_type=MESH,
    )
    halo.start()
    pend = []

    GD = {}

    def ggo(i, h, e, src, dst, chan):
        cp = remote(src, dst, gsend.at[i, h, e], grecv.at[i, h, e], chan)
        cp.start()
        GD[i, h, e] = cp

    def blk(axis, d, r0, n):
        if axis == 0:
            return G.at[y, wrap4(x + d), k, pl.ds(r0, n)]
        return G.at[wrap4(y + d), x, k, pl.ds(r0, n)]

    def gline(h, d, r0, n):
        if h == 0:
            return G.at[wrap4(y + d), :, k, pl.ds(r0, n)]
        return G.at[:, wrap4(x + d), k, pl.ds(r0, n)]

    def t0(i):
        for h in (0, 1):
            r0, n = PIECES[i][h]
            v = G.at[y, x, k, pl.ds(r0, n)]
            ggo(i, h, 0, v, v, peer(h, 1))
            ggo(i, h, 1, v, v, peer(h, -1))

    def t1(i):
        for h in (0, 1):
            r0, n = PIECES[i][h]
            a, b = half_rows(n)
            GD[i, h, 0].wait_recv()
            v = blk(h, -1, r0, a)
            ggo(i, h, 2, v, v, peer(h, 1))
            GD[i, h, 1].wait_recv()
            v = blk(h, 1, r0 + a, b)
            ggo(i, h, 3, v, v, peer(h, -1))

    def t2(i):
        for h in (0, 1):
            r0, n = PIECES[i][h]
            GD[i, h, 2].wait_recv()
            GD[i, h, 3].wait_recv()
            v = gline(h, 0, r0, n)
            ggo(i, h, 4, v, v, peer(1 - h, 1))
            ggo(i, h, 5, v, v, peer(1 - h, -1))
            ggo(i, h, 6, v, v, sib)

    def t3(i):
        for h in (0, 1):
            r0, n = PIECES[i][h]
            a, b = half_rows(n)
            GD[i, h, 4].wait_recv()
            v = gline(h, -1, r0, a)
            ggo(i, h, 7, v, v, peer(1 - h, 1))
            v = gline(h, -1, r0, n)
            ggo(i, h, 8, v, v, sib)
            GD[i, h, 5].wait_recv()
            v = gline(h, 1, r0 + a, b)
            ggo(i, h, 9, v, v, peer(1 - h, -1))
            v = gline(h, 1, r0, n)
            ggo(i, h, 10, v, v, sib)

    def t4(i):
        for h in (0, 1):
            r0, n = PIECES[i][h]
            a, b = half_rows(n)
            GD[i, h, 7].wait_recv()
            v = gline(h, 2, r0, a)
            ggo(i, h, 11, v, v, sib)
            GD[i, h, 9].wait_recv()
            v = gline(h, 2, r0 + a, b)
            ggo(i, h, 12, v, v, sib)

    def t5(i):
        for h in (0, 1):
            for e in (6, 8, 10, 11, 12):
                GD[i, h, e].wait_recv()

    def load_block(c, rows):
        return G[c // 8, (c // 2) % 4, c % 2, rows, :]

    def span(q):
        return (0, HALO + Q) if q == 0 else (HALO + q * Q, Q)

    def assemble(q):
        first, count = span(q)

        def body(r, _):
            rows = pl.ds(pl.multiple_of(first + r * 16, 16), 16)
            acc = [jnp.zeros((16, 128), F32) for _ in range(4)]
            for c in range(32):
                v = load_block(c, rows).astype(F32)
                acc[c % 4] = acc[c % 4] + v * v
                X[rows, c * 128 : (c + 1) * 128] = (v * gain_in[0:1, c * 128 : (c + 1) * 128]).astype(BF)
            SQ[rows, :] = (acc[0] + acc[1]) + (acc[2] + acc[3])
            return 0

        lax.fori_loop(0, count // 16, body, 0)
        rows = slice(first, first + count)
        total = jnp.sum(SQ[rows, :], axis=1, keepdims=True)
        inv[rows, :] = lax.rsqrt(total * (1.0 / 4096) + 1e-05)

    def state_weights():
        for cp in wcopies:
            cp.wait()
        for c in range(32):
            for j in range(3):
                W[c * 128 : (c + 1) * 128, 512 + j * 128 : 640 + j * 128] = load_block(
                    c, pl.ds(SBASE + j * 128, 128)
                )

    def project_gate(q):
        rows = slice(HALO + q * 512, HALO + q * 512 + 512)
        raw = jnp.dot(X[rows, :], W[:, 0:256], preferred_element_type=F32) * inv[rows, :]
        GT[q * 512 : q * 512 + 512, :] = raw.astype(BF)

    def project(q):
        first, count = span(q)
        rows = slice(first, first + count)
        raw = jnp.dot(X[rows, :], W[:, 256:896], preferred_element_type=F32) * inv[rows, :]
        IN[rows, :] = raw[:, 0:256].astype(BF)
        PJ[rows, :] = raw[:, 256:640]

    lane = lax.broadcasted_iota(jnp.int32, (1, 128), 1)

    def lanes(ref):
        row = jnp.zeros((1, 128), F32)
        for h in range(4):
            row = jnp.where(lane == h, ref[h], row)
        return row

    def wide(v):
        return jnp.concatenate(
            [jnp.where(lane < 64, v[:, 0:1], v[:, 1:2]), jnp.where(lane < 64, v[:, 2:3], v[:, 3:4])],
            axis=1,
        )

    bias_row = lanes(rate_bias)
    rate_row = jnp.where(lane < 4, -jnp.exp(lanes(log_rate)), 0.0)
    skip_row = wide(lanes(skip))
    shift = lax.rem(128 - 4 * lax.axis_index("chan"), 128)
    lower = lax.broadcasted_iota(jnp.int32, (Q, Q), 0) >= lax.broadcasted_iota(jnp.int32, (Q, Q), 1)

    def silu(v):
        return v / (1.0 + jnp.exp(-v))

    def mix(v, w):
        total = w[0:1, :] * v[13 : 13 + Q]
        for j in range(1, K):
            total = total + w[j : j + 1, :] * v[13 + j : 13 + j + Q]
        return silu(total)

    def softplus(v):
        u = jnp.exp(-jnp.abs(v))
        small = u * (1.0 + u * (-0.5 + u * (1.0 / 3 + u * (-0.25 + u * 0.2))))
        return jnp.maximum(v, 0.0) + jnp.where(u < 0.03, small, jnp.log(1.0 + u))

    def split3(v):
        hi = v.astype(BF)
        rest = v - hi.astype(F32)
        mid = rest.astype(BF)
        return hi, mid, (rest - mid.astype(F32)).astype(BF)

    SE[0] = jnp.zeros((N, 256), F32)
    BE[0] = jnp.zeros((8, 128), F32)
    tri = lower.astype(F32).astype(BF)

    def states(b):
        r0 = b * Q
        rows = pl.ds(r0, Q)
        xs = mix(IN[pl.ds(r0, Q + HALO), :].astype(F32), cw[...])
        XC[rows, :] = xs
        maps = mix(PJ[pl.ds(r0, Q + HALO), 0:256], cs[...]).astype(BF)
        BC[rows, :] = maps
        rate = pltpu.roll(PJ[pl.ds(r0 + HALO, Q), 256:384], shift, 1)
        step = softplus(rate + bias_row)
        decay = rate_row * step
        within = jnp.zeros((Q, 128), F32)
        for part in split3(decay):
            within = within + jnp.dot(tri, part, preferred_element_type=F32)
        DT[rows, :] = step
        WI[rows, :] = within
        last = within[Q - 1 : Q, :]
        BE[b + 1] = BE[b] + last
        weighted = (xs * wide(jnp.exp(last - within) * step)).astype(BF)
        fresh = lax.dot_general(
            maps[:, 0:N], weighted, (((0,), (0,)), ((), ())), preferred_element_type=F32
        )
        SE[b + 1] = wide(jnp.exp(last)) * SE[b] + fresh

    def inside(b):
        rows = pl.ds(b * Q, Q)
        xs = XC[rows, :]
        xb = xs.astype(BF)
        im, om = BC[rows, 0:N], BC[rows, N:]
        within, step = WI[rows, :], DT[rows, :]
        scores = lax.dot_general(om, im, (((1,), (1,)), ((), ())), preferred_element_type=F32)
        within_t, step_t = within.T, step.T
        parts = []
        for h in range(4):
            gap = within[:, h : h + 1] - within_t[h : h + 1, :]
            fading = jnp.exp(jnp.where(lower, gap, -1e30))
            mixing = (scores * fading * step_t[h : h + 1, :]).astype(BF)
            pair = h // 2
            parts.append(
                jnp.dot(mixing, xb[:, pair * 128 : (pair + 1) * 128], preferred_element_type=F32)
            )
        near = jnp.concatenate(
            [jnp.where(lane < 64, parts[0], parts[1]), jnp.where(lane < 64, parts[2], parts[3])],
            axis=1,
        )
        far = jnp.dot(om, SE[b].astype(BF), preferred_element_type=F32)
        opened = silu(GT[rows, :].astype(F32))
        Y[rows, :] = (near + far * wide(jnp.exp(within)) + skip_row * xs) * opened
        EG[rows, :] = wide(jnp.exp(BE[b][0:1, :] + within)) * opened

    ZD = {}

    def zgo(way, s, j):
        at = lax.rem(z - s + 9, 8) if way == 0 else lax.rem(z + s - 1, 8)
        to = lax.rem(z + 1, 8) if way == 0 else lax.rem(z + 7, 8)
        cp = pltpu.make_async_remote_copy(
            src_ref=ZB.at[at, j], dst_ref=ZB.at[at, j],
            send_sem=zsem.at[0, way, s - 1, j], recv_sem=zsem.at[1, way, s - 1, j],
            device_id={"seq": to}, device_id_type=MESH,
        )
        cp.start()
        ZD[way, s, j] = cp
        pend.append(cp)

    def zstep(s):
        for j in range(2):
            for way in range(2):
                if s > 1:
                    ZD[way, s - 1, j].wait_recv()
                if s < 4 or j == way:
                    zgo(way, s, j)

    def zstart():
        sub = lax.broadcasted_iota(jnp.int32, (16, 128), 0)
        total_row = wide(BE[4][0:1, :])
        for j in range(2):
            cols = slice(j * 128, (j + 1) * 128)
            ZB[z, j, 0:N, :] = SE[4, :, cols].astype(BF)
            hi, mid, lo = [p.astype(F32) for p in split3(total_row[:, cols])]
            ZB[z, j, N : N + 16, :] = jnp.where(
                sub == 0, hi, jnp.where(sub == 1, mid, jnp.where(sub == 2, lo, 0.0))
            ).astype(BF)

    for cp in own[1:]:
        cp.wait()
    t0(0)
    own[0].wait()
    halo.wait_recv()

    @pl.when(z == 0)
    def _():
        G[y, x, k, pl.ds(0, HALO), :] = jnp.zeros((HALO, 128), BF)

    t0(1)

    local = []
    wrem = []
    for j in range(16):
        col = pl.multiple_of((2 * j + k) * 128, 128)
        cp = pltpu.make_async_copy(
            outp.at[:, pl.ds(col, 128)], Wo.at[pl.ds(0, 256), pl.ds(j * 128, 128)], lsem.at[j]
        )
        cp.start()
        local.append(cp)
        col = pl.multiple_of((2 * j + 1 - k) * 128, 128)
        cp = remote(
            outp.at[:, pl.ds(col, 128)], Wo.at[pl.ds(256, 256), pl.ds(j * 128, 128)],
            wsem.at[0, j], wsem.at[1, j], sib,
        )
        cp.start()
        wrem.append(cp)

    for name, i in (
        (1, 0), (0, 2), (0, 3), (0, 4), (1, 1), (2, 0), (1, 2), (2, 1), (1, 3), (1, 4),
        (3, 0), (2, 2), (3, 1), (2, 3), (4, 0), (5, 0), (6, 0), (3, 2), (2, 4), (4, 1), (5, 1),
        (7, 0), (8, 0), (3, 3), (9, 0), (4, 2), (5, 2), (7, 1), (3, 4), (8, 1), (9, 1), (4, 3), (4, 4),
        (5, 3), (7, 2), (8, 2), (9, 2), (5, 4), (7, 3), (8, 3), (9, 3),
    ):
        if name == 6:
            state_weights()
        else:
            (t0, t1, t2, t3, t4, t5, None, assemble, project, states)[name](i)
    zstart()
    zstep(1)
    project_gate(0)
    inside(0)
    zstep(2)
    inside(1)
    project_gate(1)
    zstep(3)
    inside(2)
    inside(3)
    zstep(4)
    ZD[0, 4, 0].wait_recv()
    ZD[1, 4, 1].wait_recv()

    halves = []
    for j in range(2):
        state = jnp.zeros((N, 128), F32)
        for s in range(7):
            tail = ZB[s, j, N : N + 16, :].astype(F32)
            fade = jnp.exp(tail[0:1] + tail[1:2] + tail[2:3])
            longer = state * fade + ZB[s, j, 0:N, :].astype(F32)
            state = jnp.where(s < z, longer, state)
        halves.append(state)
    carried = jnp.concatenate(halves, axis=1).astype(BF)

    grem = []
    ones = jnp.ones((8, 256), BF)

    def finish(q):
        rows = pl.ds(q * Q, Q)
        v = Y[rows, :] + jnp.dot(BC[rows, N:], carried, preferred_element_type=F32) * EG[rows, :]
        g[0, rows, :] = (v * gain[...]).astype(BF)
        cp = remote(g.at[0, rows], g.at[1, rows], gsem.at[0, q], gsem.at[1, q], sib)
        cp.start()
        grem.append(cp)
        total = jnp.zeros((8, Q), F32)
        for part in split3(v * v)[:2]:
            total = total + lax.dot_general(
                ones, part, (((1,), (1,)), ((), ())), preferred_element_type=F32
            )
        EO[0, :, q * Q : (q + 1) * Q] = total

    def line(qh, h, d):
        if h == 0:
            return PP.at[qh, :, wrap4(x + d)]
        return PP.at[qh, wrap4(y + d)]

    D = {}

    def go(qh, e, src, dst, chan):
        cp = remote(src, dst, send.at[qh, e], recv.at[qh, e], chan)
        cp.start()
        D[qh, e] = cp

    def u0(qh):
        h = qh % 2
        rows = pl.ds(qh * 128, 128)
        both = jnp.concatenate([g[0, rows, :], g[1, rows, :]], axis=1)
        for n in range(4):
            acc = jnp.dot(both, Wo[:, n * 512 : (n + 1) * 512], preferred_element_type=F32)
            for m in range(4):
                PP[qh, n, m] = acc[:, m * 128 : (m + 1) * 128]
        far = line(qh, h, 2)
        SA[qh, 0] = far[:, 0:64, :].astype(BF)
        go(qh, 0, SA.at[qh, 0], RA.at[qh, 0], peer(h, 1))
        SA[qh, 1] = far[:, 64:128, :].astype(BF)
        go(qh, 1, SA.at[qh, 1], RA.at[qh, 1], peer(h, -1))

    def u1(qh):
        h = qh % 2
        D[qh, 0].wait_recv()
        v = line(qh, h, 1)
        SB[qh, 0, :, 0:64] = (v[:, 0:64, :] + RA[qh, 0].astype(F32)).astype(BF)
        SB[qh, 0, :, 64:128] = v[:, 64:128, :].astype(BF)
        go(qh, 2, SB.at[qh, 0], RB.at[qh, 0], peer(h, 1))
        D[qh, 1].wait_recv()
        v = line(qh, h, -1)
        SB[qh, 1, :, 0:64] = v[:, 0:64, :].astype(BF)
        SB[qh, 1, :, 64:128] = (v[:, 64:128, :] + RA[qh, 1].astype(F32)).astype(BF)
        go(qh, 3, SB.at[qh, 1], RB.at[qh, 1], peer(h, -1))

    def u2(qh):
        h = qh % 2
        D[qh, 2].wait_recv()
        D[qh, 3].wait_recv()
        LS[qh] = line(qh, h, 0)[...] + RB[qh, 0].astype(F32) + RB[qh, 1].astype(F32)
        at = y if h == 0 else x
        far = LS.at[qh, wrap4(at + 2)]
        SC[qh, 0] = far[0:64, :].astype(BF)
        go(qh, 4, SC.at[qh, 0], RC.at[qh, 0], peer(1 - h, 1))
        SC[qh, 1] = far[64:128, :].astype(BF)
        go(qh, 5, SC.at[qh, 1], RC.at[qh, 1], peer(1 - h, -1))

    def u3(qh):
        h = qh % 2
        at = y if h == 0 else x
        D[qh, 4].wait_recv()
        v = LS.at[qh, wrap4(at + 1)]
        SD[qh, 0, 0:64] = (v[0:64, :] + RC[qh, 0].astype(F32)).astype(BF)
        SD[qh, 0, 64:128] = v[64:128, :].astype(BF)
        go(qh, 6, SD.at[qh, 0], RD.at[qh, 0], peer(1 - h, 1))
        D[qh, 5].wait_recv()
        v = LS.at[qh, wrap4(at - 1)]
        SD[qh, 1, 0:64] = v[0:64, :].astype(BF)
        SD[qh, 1, 64:128] = (v[64:128, :] + RC[qh, 1].astype(F32)).astype(BF)
        go(qh, 7, SD.at[qh, 1], RD.at[qh, 1], peer(1 - h, -1))

    def u4(qh):
        h = qh % 2
        at = y if h == 0 else x
        D[qh, 6].wait_recv()
        D[qh, 7].wait_recv()
        total = LS[qh, at] + RD[qh, 0].astype(F32) + RD[qh, 1].astype(F32)
        rows = pl.ds(qh * 128, 128)
        out[rows, :] = (tok[rows, :].astype(F32) + total * scale[rows, :]).astype(BF)

    def energy(stage):
        if stage == 0:
            e0.wait_recv()
            EO[1] = EO[0] + ER[0]
        else:
            for d in (1, 2, 3):
                erem[stage - 1][d - 1].wait_recv()
            EO[stage + 1] = EO[stage] + ER[3 * stage - 2] + ER[3 * stage - 1] + ER[3 * stage]
        if stage < 2:
            cps = []
            for d in (1, 2, 3):
                s = 3 * stage + d
                cp = remote(EO.at[stage + 1], ER.at[s], esem.at[0, s], esem.at[1, s], peer(stage, d))
                cp.start()
                cps.append(cp)
            erem.append(cps)
            pend.extend(cps)
        else:
            factor = lax.rsqrt(EO[3] * (1.0 / DI) + 1e-05)
            one = jnp.where(lax.broadcasted_iota(jnp.int32, (8, 128), 0) == 0, 1.0, 0.0).astype(F32)
            scale[...] = lax.dot_general(
                factor, one, (((0,), (0,)), ((), ())),
                preferred_element_type=F32, precision=lax.Precision.HIGHEST,
            )

    erem = []
    for cp in local:
        cp.wait()
    for cp in wrem:
        cp.wait_recv()
    finish(0)
    finish(1)
    for q in range(4):
        grem[q].wait_recv()
        u0(2 * q)
        u0(2 * q + 1)
        if q < 2:
            finish(q + 2)
        if q == 1:
            e0 = remote(EO.at[0], ER.at[0], esem.at[0, 0], esem.at[1, 0], sib)
            e0.start()
            pend.append(e0)
        if q == 2:
            u1(0)
            u1(1)
    energy(0)
    for name, q in (
        (1, 1), (1, 2), (2, 0), (1, 3), (5, 1), (2, 1), (2, 2), (2, 3), (5, 2), (3, 0), (3, 1), (3, 2), (3, 3),
        (4, 0), (4, 1), (4, 2), (4, 3),
    ):
        if name == 5:
            energy(q)
        else:
            fn = (u1, u2, u3, u4)[name - 1]
            fn(2 * q)
            fn(2 * q + 1)
    halo.wait_send()
    for cp in wrem + grem + pend + list(GD.values()) + list(D.values()):
        cp.wait_send()


def vspec():
    return pl.BlockSpec(memory_space=pltpu.VMEM)


def sspec():
    return pl.BlockSpec(memory_space=pltpu.SMEM)


def aspec():
    return pl.BlockSpec(memory_space=pl.ANY)


def local(
    tokens, norm_gain, gate_proj, inner_proj, state_proj, conv_inner, conv_state,
    log_rate, rate_bias, skip_gain, gate_gain, out_proj,
):
    big = lambda *s: pltpu.VMEM(s, BF)
    full = lambda *s: pltpu.VMEM(s, F32)
    dma = lambda *s: pltpu.SemaphoreType.DMA(s)
    return pl.pallas_call(
        layer_kernel,
        name="layer",
        out_shape=jax.ShapeDtypeStruct((ROWS, 128), BF),
        in_specs=[vspec()] * 3 + [aspec()] * 2 + [vspec()] * 2 + [sspec()] * 3 + [vspec(), aspec()],
        out_specs=vspec(),
        scratch_shapes=[
            big(4, 4, 2, GROWS, 128),
            big(ROWS + HALO, 4096),
            big(4096, 896),
            full(ROWS + HALO, 128),
            full(ROWS + HALO, 1),
            big(ROWS + HALO, 256),
            full(ROWS + HALO, SROWS),
            big(ROWS, 256),
            big(2, ROWS, 256),
            big(512, 2048),
            full(NQ, 4, 4, 128, 128),
            full(NQ, 4, 128, 128),
            big(NQ, 2, 4, 64, 128),
            big(NQ, 2, 4, 128, 128),
            big(NQ, 2, 64, 128),
            big(NQ, 2, 128, 128),
            big(NQ, 2, 4, 64, 128),
            big(NQ, 2, 4, 128, 128),
            big(NQ, 2, 64, 128),
            big(NQ, 2, 128, 128),
            full(4, 8, ROWS),
            full(7, 8, ROWS),
            full(ROWS, 128),
            full(ROWS, 256),
            big(ROWS, 256),
            full(ROWS, 128),
            full(ROWS, 128),
            full(5, 8, 128),
            full(5, N, 256),
            full(ROWS, 256),
            full(ROWS, 256),
            big(8, 2, N + 16, 128),
            dma(NP, 2, 13),
            dma(NP, 2, 13),
            dma(2),
            dma(6),
            dma(NQ, 8),
            dma(NQ, 8),
            dma(2, 4),
            dma(2, 16),
            dma(16),
            dma(2, 7),
            dma(2, 2, 4, 2),
        ],
        compiler_params=pltpu.CompilerParams(
            collective_id=0, has_side_effects=True, vmem_limit_bytes=VLIM
        ),
    )(
        tokens, state_proj, norm_gain.reshape(1, -1), gate_proj, inner_proj, conv_inner, conv_state,
        log_rate, rate_bias, skip_gain, gate_gain.reshape(1, -1), out_proj,
    )


def solution(mesh):
    return jax.shard_map(
        local,
        mesh=mesh,
        in_specs=(
            P("seq", "chan"),
            P(),
            P(None, "chan"),
            P(None, "chan"),
            P("chan", None),
            P(None, "chan"),
            P(),
            P("chan"),
            P("chan"),
            P("chan"),
            P("chan"),
            P("chan", None),
        ),
        out_specs=P("seq", "chan"),
        check_vma=False,
    )
```

time: 187 us -> 105 us (0.56)
  waiting for transfers between devices: 18.6 us -> 0 us
  local copies, waits for them, and re-layouts: 20.2 us -> 1.67 us
  blocking collectives: 14.3 us -> 0 us
  between operations: 13.6 us -> 0.01 us
  other arithmetic: 8.85 us -> 0 us
  matrix products: 7.19 us -> 0 us
  Pallas kernels: 103 us -> 101 us
    all_gather x1 -> x0, waiting for transfers between devices: 18.5 us -> none  [prefix(): pieces = jax.tree.map(lambda part: lax.all_gather(part, axis), value)]
    all_gather x1 -> x0, blocking collectives: 14.3 us -> none  [prefix(): pieces = jax.tree.map(lambda part: lax.all_gather(part, axis), value)]
    mul x6 -> x0, other arithmetic: 7.32 us -> none  [the longest x1 3.29 us: local(): gated_out = ssd_out * jax.nn.silu(gate_raw.astype(jnp.float32))]
    dynamic_slice x14 -> x0, local copies, waits for them, and re-layouts: 7.32 us -> none  [turn(): longer = join(total, jax.tree.map(lambda part: part[position], pieces))]
    reshape x5 -> x0, local copies, waits for them, and re-layouts: 6.98 us -> none  [the longest x2 3.95 us: local(): (local_out + carried_out).reshape(token_rows, heads * P_SIZE)]
    dot_general x5 -> x0, matrix products: 6.9 us -> none  [the longest x1 2.36 us: local(): local_out = jnp.einsum('chts,cshp->cthp', mixing, values)]
    mul x10 -> x0, local copies, waits for them, and re-layouts: 2.81 us -> none  [the longest x1 2.65 us: causal_mix(): return jax.nn.silu(summed)]
    pallas_call x2 -> x1, Pallas kernels: 103 us -> 101 us  [local(): pl.pallas_call(layer_kernel, name='layer', out_shape=jax.ShapeDtypeStruct...]
  transfers between devices with their start and end apart: 1 -> 0, of which waited for: 1 -> 0; matrix products, arithmetic and copies ran while one was open for 1% -> 0% of each run, Pallas kernels for 0% -> 0%
where the time goes in v3:
time: 105 us; the launch traced here: 103 us
  Pallas kernels  101 us (96%)
  local copies, waits for them, and re-layouts  1.67 us (2%)
    pallas_call x1, Pallas kernels, local(): pl.pallas_call(layer_kernel, name='layer', out_shape=jax.ShapeDtypeStruct...  101 us

profile of v3, /device:TPU:2, one launch (start us, length us, event | category | flops | bytes accessed | tf_op | source)
XLA Modules:
  0.0 103.1 jit_solution(8870671699129017452)
XLA Ops:
  0.0 101.4 %layer.1 = bf16[1024,128]{1,0:T(8,128)(2,1)} custom-call(bf16[1024,128]{1,0:T(8,128)(2,1)} %tok.1, bf16[128,384]{1,0:T(8,128)(2,1)} %stp.1, f32[1,4096]{1,0:T(1,128)} %bitcast.2, bf16[4096,256]{1,0:T(8,128)(2,1)} %gate_hbm.1, bf16[4096,256]{1,0:T(8,128)(2,1)} %inner_hbm.1, f32[4,256]{1,0:T(4,128)} %cw.1, f32[4,256]{1,0:T(4,128)} %cs.1, f32[4]{0:T(128)} %log_rate.1, ...), custom_call_target="tpu_custom_call" | custom-call | tf_op jit(solution)/shard_map/layer/pallas_call | solution.py:588
  101.4 1.7 %copy.14 = bf16[1024,128]{1,0:T(8,128)(2,1)} copy(bf16[1024,128]{1,0:T(8,128)(2,1)} %layer.1) | data formatting | bytes 524288

commit v4 on v3

--- a/solution.py
+++ b/solution.py
@@ -46,10 +46,12 @@
 SBASE = HALO + ROWS
 GROWS = SBASE + SROWS
 NQ = 8
-PIECES = [((SBASE, 192), (SBASE + 192, 192)), ((0, 144), (144, 128))] + [
-    ((HALO + q * 256, 128), (HALO + q * 256 + 128, 128)) for q in (1, 2, 3)
+PIECES = [((SBASE, 192), (SBASE + 192, 192)), ((272, 128), (400, 128)), ((0, 144), (144, 128))] + [
+    ((HALO + q * 256, 128), (HALO + q * 256 + 128, 128)) for q in (2, 3)
 ]
 NP = len(PIECES)
+STAGES = (0, 0, 1, 1, 2, 2, 4, 3, 4, 3, 4, 4, 4)
+SENDS = (0, 0, 0, 0, 1, 2, 3, 4, 5, 4, 6, 7, 7)
 
 
 def half_rows(n):
@@ -62,8 +64,7 @@
     G, X, W, SQ, inv, IN, PJ, GT,
     g, Wo, PP, LS, SA, SB, SC, SD, RA, RB, RC, RD, EO, ER, scale,
     XC, BC, WI, DT, BE, SE, Y, EG, ZB,
-    gsend, grecv, hsem, osem,
-    send, recv, gsem, wsem, lsem, esem, zsem,
+    res, gsend, grecv, send, recv, sems,
 ):
     y, x, k = place()
     z = lax.axis_index("seq")
@@ -73,16 +74,16 @@
 
     sib = chan_id(y, x, 1 - k)
 
-    own = [pltpu.make_async_copy(tok, G.at[y, x, k, pl.ds(HALO, ROWS)], osem.at[0])]
+    own = [pltpu.make_async_copy(tok, G.at[y, x, k, pl.ds(HALO, ROWS)], sems.at[2])]
     for j in range(3):
         own.append(
             pltpu.make_async_copy(
-                stp.at[:, pl.ds(j * 128, 128)], G.at[y, x, k, pl.ds(SBASE + j * 128, 128)], osem.at[1 + j]
+                stp.at[:, pl.ds(j * 128, 128)], G.at[y, x, k, pl.ds(SBASE + j * 128, 128)], sems.at[3]
             )
         )
     wcopies = [
-        pltpu.make_async_copy(gate_hbm, W.at[:, 0:256], osem.at[4]),
-        pltpu.make_async_copy(inner_hbm, W.at[:, 256:512], osem.at[5]),
+        pltpu.make_async_copy(gate_hbm, W.at[:, 0:256], sems.at[4]),
+        pltpu.make_async_copy(inner_hbm, W.at[:, 256:512], sems.at[4]),
     ]
     for cp in own + wcopies:
         cp.start()
@@ -95,20 +96,23 @@
     pl.semaphore_wait(bar, 9)
 
     halo = pltpu.make_async_remote_copy(
-        src_ref=tok.at[pl.ds(ROWS - HALO, HALO)],
+        src_ref=G.at[y, x, k, pl.ds(ROWS, HALO)],
         dst_ref=G.at[y, x, k, pl.ds(0, HALO)],
-        send_sem=hsem.at[0], recv_sem=hsem.at[1],
+        send_sem=sems.at[0], recv_sem=sems.at[1],
         device_id={"seq": lax.rem(z + 1, 8)}, device_id_type=MESH,
     )
-    halo.start()
-    pend = []
-
-    GD = {}
 
     def ggo(i, h, e, src, dst, chan):
-        cp = remote(src, dst, gsend.at[i, h, e], grecv.at[i, h, e], chan)
-        cp.start()
-        GD[i, h, e] = cp
+        remote(src, dst, gsend.at[SENDS[e]], grecv.at[i, STAGES[e]], chan).start()
+
+    def gwait(i, stage):
+        (r0, a), (_, b) = PIECES[i]
+        rows = pl.ds(r0, a + b)
+        ref = (
+            G.at[0, pl.ds(0, 2), 0, rows], G.at[0, 0, 0, rows], G.at[pl.ds(0, 2), :, 0, rows],
+            G.at[0, :, 0, rows], G.at[:, :, 0, rows],
+        )[stage]
+        remote(ref, ref, gsend.at[0], grecv.at[i, stage], sib).wait_recv()
 
     def blk(axis, d, r0, n):
         if axis == 0:
@@ -128,56 +132,50 @@
             ggo(i, h, 1, v, v, peer(h, -1))
 
     def t1(i):
+        gwait(i, 0)
         for h in (0, 1):
             r0, n = PIECES[i][h]
             a, b = half_rows(n)
-            GD[i, h, 0].wait_recv()
             v = blk(h, -1, r0, a)
             ggo(i, h, 2, v, v, peer(h, 1))
-            GD[i, h, 1].wait_recv()
             v = blk(h, 1, r0 + a, b)
             ggo(i, h, 3, v, v, peer(h, -1))
 
     def t2(i):
+        gwait(i, 1)
         for h in (0, 1):
             r0, n = PIECES[i][h]
-            GD[i, h, 2].wait_recv()
-            GD[i, h, 3].wait_recv()
             v = gline(h, 0, r0, n)
             ggo(i, h, 4, v, v, peer(1 - h, 1))
             ggo(i, h, 5, v, v, peer(1 - h, -1))
             ggo(i, h, 6, v, v, sib)
 
     def t3(i):
+        gwait(i, 2)
         for h in (0, 1):
             r0, n = PIECES[i][h]
             a, b = half_rows(n)
-            GD[i, h, 4].wait_recv()
             v = gline(h, -1, r0, a)
             ggo(i, h, 7, v, v, peer(1 - h, 1))
             v = gline(h, -1, r0, n)
             ggo(i, h, 8, v, v, sib)
-            GD[i, h, 5].wait_recv()
             v = gline(h, 1, r0 + a, b)
             ggo(i, h, 9, v, v, peer(1 - h, -1))
             v = gline(h, 1, r0, n)
             ggo(i, h, 10, v, v, sib)
 
     def t4(i):
+        gwait(i, 3)
         for h in (0, 1):
             r0, n = PIECES[i][h]
             a, b = half_rows(n)
-            GD[i, h, 7].wait_recv()
             v = gline(h, 2, r0, a)
             ggo(i, h, 11, v, v, sib)
-            GD[i, h, 9].wait_recv()
             v = gline(h, 2, r0 + a, b)
             ggo(i, h, 12, v, v, sib)
 
     def t5(i):
-        for h in (0, 1):
-            for e in (6, 8, 10, 11, 12):
-                GD[i, h, e].wait_recv()
+        gwait(i, 4)
 
     def load_block(c, rows):
         return G[c // 8, (c // 2) % 4, c % 2, rows, :]
@@ -204,8 +202,7 @@
         inv[rows, :] = lax.rsqrt(total * (1.0 / 4096) + 1e-05)
 
     def state_weights():
-        for cp in wcopies:
-            cp.wait()
+        pltpu.make_async_copy(W.at[:, 0:512], W.at[:, 0:512], sems.at[4]).wait()
         for c in range(32):
             for j in range(3):
                 W[c * 128 : (c + 1) * 128, 512 + j * 128 : 640 + j * 128] = load_block(
@@ -213,9 +210,9 @@
                 )
 
     def project_gate(q):
-        rows = slice(HALO + q * 512, HALO + q * 512 + 512)
+        rows = slice(HALO + q * Q, HALO + q * Q + Q)
         raw = jnp.dot(X[rows, :], W[:, 0:256], preferred_element_type=F32) * inv[rows, :]
-        GT[q * 512 : q * 512 + 512, :] = raw.astype(BF)
+        GT[q * Q : q * Q + Q, :] = raw.astype(BF)
 
     def project(q):
         first, count = span(q)
@@ -317,27 +314,26 @@
         Y[rows, :] = (near + far * wide(jnp.exp(within)) + skip_row * xs) * opened
         EG[rows, :] = wide(jnp.exp(BE[b][0:1, :] + within)) * opened
 
-    ZD = {}
-
     def zgo(way, s, j):
         at = lax.rem(z - s + 9, 8) if way == 0 else lax.rem(z + s - 1, 8)
         to = lax.rem(z + 1, 8) if way == 0 else lax.rem(z + 7, 8)
         cp = pltpu.make_async_remote_copy(
             src_ref=ZB.at[at, j], dst_ref=ZB.at[at, j],
-            send_sem=zsem.at[0, way, s - 1, j], recv_sem=zsem.at[1, way, s - 1, j],
+            send_sem=sems.at[18], recv_sem=sems.at[19 + (s - 1) * 2 + j],
             device_id={"seq": to}, device_id_type=MESH,
         )
         cp.start()
-        ZD[way, s, j] = cp
-        pend.append(cp)
-
-    def zstep(s):
-        for j in range(2):
-            for way in range(2):
-                if s > 1:
-                    ZD[way, s - 1, j].wait_recv()
-                if s < 4 or j == way:
-                    zgo(way, s, j)
+
+    def zwait(s, j):
+        ref = ZB.at[pl.ds(0, 2 if s < 4 else 1), j]
+        remote(ref, ref, sems.at[18], sems.at[19 + (s - 1) * 2 + j], sib).wait_recv()
+
+    def zstep(s, j):
+        if s > 1:
+            zwait(s - 1, j)
+        for way in range(2):
+            if s < 4 or j == way:
+                zgo(way, s, j)
 
     def zstart():
         sub = lax.broadcasted_iota(jnp.int32, (16, 128), 0)
@@ -350,58 +346,69 @@
                 sub == 0, hi, jnp.where(sub == 1, mid, jnp.where(sub == 2, lo, 0.0))
             ).astype(BF)
 
-    for cp in own[1:]:
-        cp.wait()
+    def first_rows():
+        halo.wait_recv()
+
+        @pl.when(z == 0)
+        def _():
+            G[y, x, k, pl.ds(0, HALO), :] = jnp.zeros((HALO, 128), BF)
+
+        for i in (2, 3, 4):
+            t0(i)
+
+    mine = G.at[y, x, k, pl.ds(SBASE, SROWS)]
+    pltpu.make_async_copy(mine, mine, sems.at[3]).wait()
     t0(0)
     own[0].wait()
-    halo.wait_recv()
-
-    @pl.when(z == 0)
-    def _():
-        G[y, x, k, pl.ds(0, HALO), :] = jnp.zeros((HALO, 128), BF)
-
+    halo.start()
     t0(1)
 
-    local = []
-    wrem = []
     for j in range(16):
+        at = pl.ds(j * 128, 128)
         col = pl.multiple_of((2 * j + k) * 128, 128)
-        cp = pltpu.make_async_copy(
-            outp.at[:, pl.ds(col, 128)], Wo.at[pl.ds(0, 256), pl.ds(j * 128, 128)], lsem.at[j]
-        )
-        cp.start()
-        local.append(cp)
+        pltpu.make_async_copy(
+            outp.at[:, pl.ds(col, 128)], Wo.at[pl.ds(0, 256), at], sems.at[13]
+        ).start()
         col = pl.multiple_of((2 * j + 1 - k) * 128, 128)
-        cp = remote(
-            outp.at[:, pl.ds(col, 128)], Wo.at[pl.ds(256, 256), pl.ds(j * 128, 128)],
-            wsem.at[0, j], wsem.at[1, j], sib,
-        )
-        cp.start()
-        wrem.append(cp)
-
+        remote(
+            outp.at[:, pl.ds(col, 128)], Wo.at[pl.ds(256, 256), at], sems.at[11], sems.at[12], sib
+        ).start()
+
+    GATE, FIRST, SW, AS, PR, ST = 5, 6, 7, 8, 9, 10
     for name, i in (
-        (1, 0), (0, 2), (0, 3), (0, 4), (1, 1), (2, 0), (1, 2), (2, 1), (1, 3), (1, 4),
-        (3, 0), (2, 2), (3, 1), (2, 3), (4, 0), (5, 0), (6, 0), (3, 2), (2, 4), (4, 1), (5, 1),
-        (7, 0), (8, 0), (3, 3), (9, 0), (4, 2), (5, 2), (7, 1), (3, 4), (8, 1), (9, 1), (4, 3), (4, 4),
-        (5, 3), (7, 2), (8, 2), (9, 2), (5, 4), (7, 3), (8, 3), (9, 3),
+        (1, 0), (FIRST, 0), (1, 1), (2, 0), (1, 2), (2, 1), (1, 3), (1, 4),
+        (3, 0), (2, 2), (3, 1), (2, 3), (4, 0), (SW, 0), (3, 2), (2, 4), (4, 1),
+        (AS, 1), (3, 3), (PR, 1), (4, 2), (GATE, 1), (AS, 0), (3, 4), (PR, 0), (4, 3), (ST, 0), (4, 4), (ST, 1),
+        (AS, 2), (PR, 2), (ST, 2), (AS, 3), (PR, 3), (ST, 3),
     ):
-        if name == 6:
+        if name == SW:
+            t5(0)
             state_weights()
+        elif name == FIRST:
+            first_rows()
         else:
-            (t0, t1, t2, t3, t4, t5, None, assemble, project, states)[name](i)
+            if name == AS:
+                t5((2, 1, 3, 4)[i])
+            (t0, t1, t2, t3, t4, project_gate, None, None, assemble, project, states)[name](i)
+
     zstart()
-    zstep(1)
+    zstep(1, 0)
+    zstep(1, 1)
+    inside(1)
     project_gate(0)
     inside(0)
-    zstep(2)
-    inside(1)
-    project_gate(1)
-    zstep(3)
+    zstep(2, 0)
+    zstep(2, 1)
+    project_gate(2)
+    zstep(3, 0)
     inside(2)
+    zstep(3, 1)
+    project_gate(3)
+    zstep(4, 0)
     inside(3)
-    zstep(4)
-    ZD[0, 4, 0].wait_recv()
-    ZD[1, 4, 1].wait_recv()
+    zstep(4, 1)
+    zwait(4, 0)
+    zwait(4, 1)
 
     halves = []
     for j in range(2):
@@ -414,16 +421,13 @@
         halves.append(state)
     carried = jnp.concatenate(halves, axis=1).astype(BF)
 
-    grem = []
     ones = jnp.ones((8, 256), BF)
 
     def finish(q):
         rows = pl.ds(q * Q, Q)
         v = Y[rows, :] + jnp.dot(BC[rows, N:], carried, preferred_element_type=F32) * EG[rows, :]
         g[0, rows, :] = (v * gain[...]).astype(BF)
-        cp = remote(g.at[0, rows], g.at[1, rows], gsem.at[0, q], gsem.at[1, q], sib)
-        cp.start()
-        grem.append(cp)
+        remote(g.at[0, rows], g.at[1, rows], sems.at[6], sems.at[7 + q], sib).start()
         total = jnp.zeros((8, Q), F32)
         for part in split3(v * v)[:2]:
             total = total + lax.dot_general(
@@ -436,12 +440,12 @@
             return PP.at[qh, :, wrap4(x + d)]
         return PP.at[qh, wrap4(y + d)]
 
-    D = {}
-
     def go(qh, e, src, dst, chan):
-        cp = remote(src, dst, send.at[qh, e], recv.at[qh, e], chan)
-        cp.start()
-        D[qh, e] = cp
+        remote(src, dst, send.at[e // 2], recv.at[qh // 2, e // 2], chan).start()
+
+    def rwait(q, stage):
+        ref = (RA, RB, RC, RD)[stage].at[pl.ds(2 * q, 2)]
+        remote(ref, ref, send.at[stage], recv.at[q, stage], sib).wait_recv()
 
     def u0(qh):
         h = qh % 2
@@ -459,12 +463,10 @@
 
     def u1(qh):
         h = qh % 2
-        D[qh, 0].wait_recv()
         v = line(qh, h, 1)
         SB[qh, 0, :, 0:64] = (v[:, 0:64, :] + RA[qh, 0].astype(F32)).astype(BF)
         SB[qh, 0, :, 64:128] = v[:, 64:128, :].astype(BF)
         go(qh, 2, SB.at[qh, 0], RB.at[qh, 0], peer(h, 1))
-        D[qh, 1].wait_recv()
         v = line(qh, h, -1)
         SB[qh, 1, :, 0:64] = v[:, 0:64, :].astype(BF)
         SB[qh, 1, :, 64:128] = (v[:, 64:128, :] + RA[qh, 1].astype(F32)).astype(BF)
@@ -472,8 +474,6 @@
 
     def u2(qh):
         h = qh % 2
-        D[qh, 2].wait_recv()
-        D[qh, 3].wait_recv()
         LS[qh] = line(qh, h, 0)[...] + RB[qh, 0].astype(F32) + RB[qh, 1].astype(F32)
         at = y if h == 0 else x
         far = LS.at[qh, wrap4(at + 2)]
@@ -485,12 +485,10 @@
     def u3(qh):
         h = qh % 2
         at = y if h == 0 else x
-        D[qh, 4].wait_recv()
         v = LS.at[qh, wrap4(at + 1)]
         SD[qh, 0, 0:64] = (v[0:64, :] + RC[qh, 0].astype(F32)).astype(BF)
         SD[qh, 0, 64:128] = v[64:128, :].astype(BF)
         go(qh, 6, SD.at[qh, 0], RD.at[qh, 0], peer(1 - h, 1))
-        D[qh, 5].wait_recv()
         v = LS.at[qh, wrap4(at - 1)]
         SD[qh, 1, 0:64] = v[0:64, :].astype(BF)
         SD[qh, 1, 64:128] = (v[64:128, :] + RC[qh, 1].astype(F32)).astype(BF)
@@ -499,71 +497,81 @@
     def u4(qh):
         h = qh % 2
         at = y if h == 0 else x
-        D[qh, 6].wait_recv()
-        D[qh, 7].wait_recv()
         total = LS[qh, at] + RD[qh, 0].astype(F32) + RD[qh, 1].astype(F32)
         rows = pl.ds(qh * 128, 128)
-        out[rows, :] = (tok[rows, :].astype(F32) + total * scale[rows, :]).astype(BF)
+        mine = G[y, x, k, pl.ds(HALO + qh * 128, 128), :].astype(F32)
+        res[rows, :] = (mine + total * scale[rows, :]).astype(BF)
+        pltpu.make_async_copy(res.at[rows], out.at[rows], sems.at[5]).start()
+
+    one = pl.ds(0, 1)
+
+    def ewait(stage):
+        ref = ER.at[pl.ds(0, 3 if stage else 1), one]
+        remote(ref, ref, sems.at[14], sems.at[15 + stage], sib).wait_recv()
 
     def energy(stage):
         if stage == 0:
-            e0.wait_recv()
-            EO[1] = EO[0] + ER[0]
+            ewait(0)
+            EO[1, one] = EO[0, one] + ER[0, one]
         else:
-            for d in (1, 2, 3):
-                erem[stage - 1][d - 1].wait_recv()
-            EO[stage + 1] = EO[stage] + ER[3 * stage - 2] + ER[3 * stage - 1] + ER[3 * stage]
+            ewait(stage)
+            first = 3 * stage - 2
+            EO[stage + 1, one] = EO[stage, one] + ER[first, one] + ER[first + 1, one] + ER[first + 2, one]
         if stage < 2:
-            cps = []
             for d in (1, 2, 3):
                 s = 3 * stage + d
-                cp = remote(EO.at[stage + 1], ER.at[s], esem.at[0, s], esem.at[1, s], peer(stage, d))
-                cp.start()
-                cps.append(cp)
-            erem.append(cps)
-            pend.extend(cps)
+                remote(
+                    EO.at[stage + 1, one], ER.at[s, one], sems.at[14], sems.at[16 + stage], peer(stage, d)
+                ).start()
         else:
-            factor = lax.rsqrt(EO[3] * (1.0 / DI) + 1e-05)
-            one = jnp.where(lax.broadcasted_iota(jnp.int32, (8, 128), 0) == 0, 1.0, 0.0).astype(F32)
+            factor = jnp.broadcast_to(lax.rsqrt(EO[3, one] * (1.0 / DI) + 1e-05), (8, ROWS))
+            pick = jnp.where(lax.broadcasted_iota(jnp.int32, (8, 128), 0) == 0, 1.0, 0.0).astype(F32)
             scale[...] = lax.dot_general(
-                factor, one, (((0,), (0,)), ((), ())),
+                factor, pick, (((0,), (0,)), ((), ())),
                 preferred_element_type=F32, precision=lax.Precision.HIGHEST,
             )
 
-    erem = []
-    for cp in local:
-        cp.wait()
-    for cp in wrem:
-        cp.wait_recv()
+    half = Wo.at[pl.ds(0, 256)]
+    pltpu.make_async_copy(half, half, sems.at[13]).wait()
+    remote(half, half, sems.at[11], sems.at[12], sib).wait_recv()
     finish(0)
     finish(1)
     for q in range(4):
-        grem[q].wait_recv()
+        theirs = g.at[1, pl.ds(q * Q, Q)]
+        remote(theirs, theirs, sems.at[6], sems.at[7 + q], sib).wait_recv()
+        if q == 3:
+            energy(0)
         u0(2 * q)
         u0(2 * q + 1)
         if q < 2:
             finish(q + 2)
         if q == 1:
-            e0 = remote(EO.at[0], ER.at[0], esem.at[0, 0], esem.at[1, 0], sib)
-            e0.start()
-            pend.append(e0)
-        if q == 2:
-            u1(0)
-            u1(1)
-    energy(0)
+            remote(EO.at[0, one], ER.at[0, one], sems.at[14], sems.at[15], sib).start()
     for name, q in (
-        (1, 1), (1, 2), (2, 0), (1, 3), (5, 1), (2, 1), (2, 2), (2, 3), (5, 2), (3, 0), (3, 1), (3, 2), (3, 3),
-        (4, 0), (4, 1), (4, 2), (4, 3),
+        (1, 0), (1, 1), (5, 1), (1, 2), (1, 3), (2, 0), (2, 1), (5, 2), (2, 2), (2, 3),
+        (3, 0), (3, 1), (3, 2), (3, 3), (4, 0), (4, 1), (4, 2), (4, 3),
     ):
         if name == 5:
             energy(q)
         else:
+            rwait(q, name - 1)
             fn = (u1, u2, u3, u4)[name - 1]
             fn(2 * q)
             fn(2 * q + 1)
-    halo.wait_send()
-    for cp in wrem + grem + pend + list(GD.values()) + list(D.values()):
-        cp.wait_send()
+    def sent(ref, sem):
+        remote(ref, ref, sem, recv.at[0, 0], sib).wait_send()
+
+    sent(G.at[0, pl.ds(0, 3), 0], gsend.at[0])
+    for e in range(1, 8):
+        sent(G.at[0, :, 0], gsend.at[e])
+    sent(G.at[0, 0, 0, pl.ds(0, HALO)], sems.at[0])
+    sent(half, sems.at[11])
+    sent(ZB.at[pl.ds(0, 7)], sems.at[18])
+    sent(g.at[0], sems.at[6])
+    sent(ER.at[pl.ds(0, 7), one], sems.at[14])
+    for stage, buf in enumerate((SA, SB, SC, SD)):
+        sent(buf, send.at[stage])
+    pltpu.make_async_copy(res, res, sems.at[5]).wait()
 
 
 def vspec():
@@ -589,8 +597,8 @@
         layer_kernel,
         name="layer",
         out_shape=jax.ShapeDtypeStruct((ROWS, 128), BF),
-        in_specs=[vspec()] * 3 + [aspec()] * 2 + [vspec()] * 2 + [sspec()] * 3 + [vspec(), aspec()],
-        out_specs=vspec(),
+        in_specs=[aspec()] * 2 + [vspec()] + [aspec()] * 2 + [vspec()] * 2 + [sspec()] * 3 + [vspec(), aspec()],
+        out_specs=aspec(),
         scratch_shapes=[
             big(4, 4, 2, GROWS, 128),
             big(ROWS + HALO, 4096),
@@ -624,17 +632,12 @@
             full(ROWS, 256),
             full(ROWS, 256),
             big(8, 2, N + 16, 128),
-            dma(NP, 2, 13),
-            dma(NP, 2, 13),
-            dma(2),
-            dma(6),
-            dma(NQ, 8),
-            dma(NQ, 8),
-            dma(2, 4),
-            dma(2, 16),
-            dma(16),
-            dma(2, 7),
-            dma(2, 2, 4, 2),
+            big(ROWS, 128),
+            dma(8),
+            dma(NP, 5),
+            dma(4),
+            dma(4, 4),
+            dma(27),
         ],
         compiler_params=pltpu.CompilerParams(
             collective_id=0, has_side_effects=True, vmem_limit_bytes=VLIM

time: 105 us -> 98.7 us (0.940); the launches traced: 103 us -> 98 us
  Pallas kernels: 101 us -> 96.4 us
    pallas_call x1, Pallas kernels: 101 us -> 96.4 us  [local(): pl.pallas_call(layer_kernel, name='layer', out_shape=jax.ShapeDtypeStruct...]
where the time goes in v4:
time: 98.7 us; the launch traced here: 98 us
  Pallas kernels  96.4 us (98%)
  local copies, waits for them, and re-layouts  1.67 us (2%)
    pallas_call x1, Pallas kernels, local(): pl.pallas_call(layer_kernel, name='layer', out_shape=jax.ShapeDtypeStruct...  96.4 us

profile of v4, /device:TPU:2, one launch (start us, length us, event | category | flops | bytes accessed | tf_op | source)
XLA Modules:
  0.0 98.0 jit_solution(5394821006278959702)
XLA Ops:
  0.0 96.4 %layer.1 = bf16[1024,128]{1,0:T(8,128)(2,1)} custom-call(bf16[1024,128]{1,0:T(8,128)(2,1)} %tok.1, bf16[128,384]{1,0:T(8,128)(2,1)} %stp.1, f32[1,4096]{1,0:T(1,128)} %bitcast.2, bf16[4096,256]{1,0:T(8,128)(2,1)} %gate_hbm.1, bf16[4096,256]{1,0:T(8,128)(2,1)} %inner_hbm.1, f32[4,256]{1,0:T(4,128)} %cw.1, f32[4,256]{1,0:T(4,128)} %cs.1, f32[4]{0:T(128)} %log_rate.1, ...), custom_call_target="tpu_custom_call" | custom-call | tf_op jit(solution)/shard_map/layer/pallas_call | solution.py:596
  96.4 1.7 %copy.14 = bf16[1024,128]{1,0:T(8,128)(2,1)} copy(bf16[1024,128]{1,0:T(8,128)(2,1)} %layer.1) | data formatting | bytes 524288

commit v5 on v4

--- a/solution.py
+++ b/solution.py
@@ -43,11 +43,11 @@
 
 ROWS = 1024
 SROWS = 384
-SBASE = HALO + ROWS
+SBASE = ROWS + HALO
 GROWS = SBASE + SROWS
 NQ = 8
-PIECES = [((SBASE, 192), (SBASE + 192, 192)), ((272, 128), (400, 128)), ((0, 144), (144, 128))] + [
-    ((HALO + q * 256, 128), (HALO + q * 256 + 128, 128)) for q in (2, 3)
+PIECES = [((0, 128), (128, 128)), ((ROWS, 208), (ROWS + 208, 192))] + [
+    ((q * 256, 128), (q * 256 + 128, 128)) for q in (1, 2, 3)
 ]
 NP = len(PIECES)
 STAGES = (0, 0, 1, 1, 2, 2, 4, 3, 4, 3, 4, 4, 4)
@@ -74,7 +74,7 @@
 
     sib = chan_id(y, x, 1 - k)
 
-    own = [pltpu.make_async_copy(tok, G.at[y, x, k, pl.ds(HALO, ROWS)], sems.at[2])]
+    own = [pltpu.make_async_copy(tok, G.at[y, x, k, pl.ds(0, ROWS)], sems.at[2])]
     for j in range(3):
         own.append(
             pltpu.make_async_copy(
@@ -96,8 +96,8 @@
     pl.semaphore_wait(bar, 9)
 
     halo = pltpu.make_async_remote_copy(
-        src_ref=G.at[y, x, k, pl.ds(ROWS, HALO)],
-        dst_ref=G.at[y, x, k, pl.ds(0, HALO)],
+        src_ref=G.at[y, x, k, pl.ds(ROWS - HALO, HALO)],
+        dst_ref=G.at[y, x, k, pl.ds(ROWS, HALO)],
         send_sem=sems.at[0], recv_sem=sems.at[1],
         device_id={"seq": lax.rem(z + 1, 8)}, device_id_type=MESH,
     )
@@ -181,7 +181,7 @@
         return G[c // 8, (c // 2) % 4, c % 2, rows, :]
 
     def span(q):
-        return (0, HALO + Q) if q == 0 else (HALO + q * Q, Q)
+        return (q * Q, Q) if q < 4 else (ROWS, HALO)
 
     def assemble(q):
         first, count = span(q)
@@ -202,7 +202,6 @@
         inv[rows, :] = lax.rsqrt(total * (1.0 / 4096) + 1e-05)
 
     def state_weights():
-        pltpu.make_async_copy(W.at[:, 0:512], W.at[:, 0:512], sems.at[4]).wait()
         for c in range(32):
             for j in range(3):
                 W[c * 128 : (c + 1) * 128, 512 + j * 128 : 640 + j * 128] = load_block(
@@ -210,16 +209,28 @@
                 )
 
     def project_gate(q):
-        rows = slice(HALO + q * Q, HALO + q * Q + Q)
+        rows = slice(q * Q, q * Q + Q)
         raw = jnp.dot(X[rows, :], W[:, 0:256], preferred_element_type=F32) * inv[rows, :]
-        GT[q * Q : q * Q + Q, :] = raw.astype(BF)
+        GT[rows, :] = raw.astype(BF)
+
+    def project_first(q):
+        rows = slice(q * Q, q * Q + Q)
+        raw = jnp.dot(X[rows, :], W[:, 0:512], preferred_element_type=F32) * inv[rows, :]
+        GT[rows, :] = raw[:, 0:256].astype(BF)
+        IN[HALO + q * Q : HALO + q * Q + Q, :] = raw[:, 256:512].astype(BF)
+
+    def project_state(q):
+        rows = slice(q * Q, q * Q + Q)
+        raw = jnp.dot(X[rows, :], W[:, 512:896], preferred_element_type=F32) * inv[rows, :]
+        PJ[HALO + q * Q : HALO + q * Q + Q, :] = raw
 
     def project(q):
         first, count = span(q)
         rows = slice(first, first + count)
+        to = slice(HALO + first, HALO + first + count) if q < 4 else slice(0, HALO)
         raw = jnp.dot(X[rows, :], W[:, 256:896], preferred_element_type=F32) * inv[rows, :]
-        IN[rows, :] = raw[:, 0:256].astype(BF)
-        PJ[rows, :] = raw[:, 256:640]
+        IN[to, :] = raw[:, 0:256].astype(BF)
+        PJ[to, :] = raw[:, 256:640]
 
     lane = lax.broadcasted_iota(jnp.int32, (1, 128), 1)
 
@@ -319,30 +330,30 @@
         to = lax.rem(z + 1, 8) if way == 0 else lax.rem(z + 7, 8)
         cp = pltpu.make_async_remote_copy(
             src_ref=ZB.at[at, j], dst_ref=ZB.at[at, j],
-            send_sem=sems.at[18], recv_sem=sems.at[19 + (s - 1) * 2 + j],
+            send_sem=sems.at[18], recv_sem=sems.at[19 + (s - 1) * 4 + j],
             device_id={"seq": to}, device_id_type=MESH,
         )
         cp.start()
 
     def zwait(s, j):
         ref = ZB.at[pl.ds(0, 2 if s < 4 else 1), j]
-        remote(ref, ref, sems.at[18], sems.at[19 + (s - 1) * 2 + j], sib).wait_recv()
+        remote(ref, ref, sems.at[18], sems.at[19 + (s - 1) * 4 + j], sib).wait_recv()
 
     def zstep(s, j):
         if s > 1:
             zwait(s - 1, j)
         for way in range(2):
-            if s < 4 or j == way:
+            if s < 4 or j // 2 == way:
                 zgo(way, s, j)
 
     def zstart():
         sub = lax.broadcasted_iota(jnp.int32, (16, 128), 0)
         total_row = wide(BE[4][0:1, :])
-        for j in range(2):
-            cols = slice(j * 128, (j + 1) * 128)
-            ZB[z, j, 0:N, :] = SE[4, :, cols].astype(BF)
+        for j in range(4):
+            half, cols = j // 2, slice((j % 2) * 128, (j % 2 + 1) * 128)
+            ZB[z, j, 0:64, :] = SE[4, half * 64 : half * 64 + 64, cols].astype(BF)
             hi, mid, lo = [p.astype(F32) for p in split3(total_row[:, cols])]
-            ZB[z, j, N : N + 16, :] = jnp.where(
+            ZB[z, j, 64:80, :] = jnp.where(
                 sub == 0, hi, jnp.where(sub == 1, mid, jnp.where(sub == 2, lo, 0.0))
             ).astype(BF)
 
@@ -351,17 +362,16 @@
 
         @pl.when(z == 0)
         def _():
-            G[y, x, k, pl.ds(0, HALO), :] = jnp.zeros((HALO, 128), BF)
-
-        for i in (2, 3, 4):
+            G[y, x, k, pl.ds(ROWS, HALO), :] = jnp.zeros((HALO, 128), BF)
+
+        for i in range(1, NP):
             t0(i)
 
+    own[0].wait()
+    halo.start()
+    t0(0)
     mine = G.at[y, x, k, pl.ds(SBASE, SROWS)]
     pltpu.make_async_copy(mine, mine, sems.at[3]).wait()
-    t0(0)
-    own[0].wait()
-    halo.start()
-    t0(1)
 
     for j in range(16):
         at = pl.ds(j * 128, 128)
@@ -374,51 +384,57 @@
             outp.at[:, pl.ds(col, 128)], Wo.at[pl.ds(256, 256), at], sems.at[11], sems.at[12], sib
         ).start()
 
-    GATE, FIRST, SW, AS, PR, ST = 5, 6, 7, 8, 9, 10
+    GATE, FIRST, SW, AS, PR, ST, PF, PS = 5, 6, 7, 8, 9, 10, 11, 12
     for name, i in (
         (1, 0), (FIRST, 0), (1, 1), (2, 0), (1, 2), (2, 1), (1, 3), (1, 4),
-        (3, 0), (2, 2), (3, 1), (2, 3), (4, 0), (SW, 0), (3, 2), (2, 4), (4, 1),
-        (AS, 1), (3, 3), (PR, 1), (4, 2), (GATE, 1), (AS, 0), (3, 4), (PR, 0), (4, 3), (ST, 0), (4, 4), (ST, 1),
-        (AS, 2), (PR, 2), (ST, 2), (AS, 3), (PR, 3), (ST, 3),
+        (3, 0), (2, 2), (3, 1), (2, 3), (4, 0), (AS, 0), (PF, 0), (3, 2), (2, 4), (4, 1),
+        (SW, 0), (AS, 4), (PR, 4), (PS, 0), (3, 3), (4, 2), (ST, 0), (AS, 1), (3, 4), (PR, 1), (4, 3), (ST, 1),
+        (AS, 2), (4, 4), (PR, 2), (ST, 2), (AS, 3), (PR, 3), (ST, 3),
     ):
         if name == SW:
-            t5(0)
+            t5(1)
             state_weights()
         elif name == FIRST:
             first_rows()
         else:
-            if name == AS:
-                t5((2, 1, 3, 4)[i])
-            (t0, t1, t2, t3, t4, project_gate, None, None, assemble, project, states)[name](i)
+            if name == AS and i < 4:
+                t5((0, 2, 3, 4)[i])
+                if i == 0:
+                    pltpu.make_async_copy(W.at[:, 0:512], W.at[:, 0:512], sems.at[4]).wait()
+            (
+                t0, t1, t2, t3, t4, project_gate, None, None, assemble, project, states,
+                project_first, project_state,
+            )[name](i)
+
+    def zsteps(s):
+        for j in range(4):
+            zstep(s, j)
 
     zstart()
-    zstep(1, 0)
-    zstep(1, 1)
+    zsteps(1)
+    inside(0)
+    project_gate(1)
+    zsteps(2)
     inside(1)
-    project_gate(0)
-    inside(0)
-    zstep(2, 0)
-    zstep(2, 1)
     project_gate(2)
-    zstep(3, 0)
+    zsteps(3)
     inside(2)
-    zstep(3, 1)
     project_gate(3)
-    zstep(4, 0)
+    zsteps(4)
     inside(3)
-    zstep(4, 1)
-    zwait(4, 0)
-    zwait(4, 1)
+    for j in range(4):
+        zwait(4, j)
 
     halves = []
-    for j in range(2):
-        state = jnp.zeros((N, 128), F32)
+    for j in range(4):
+        state = jnp.zeros((64, 128), F32)
         for s in range(7):
-            tail = ZB[s, j, N : N + 16, :].astype(F32)
+            tail = ZB[s, j, 64:80, :].astype(F32)
             fade = jnp.exp(tail[0:1] + tail[1:2] + tail[2:3])
-            longer = state * fade + ZB[s, j, 0:N, :].astype(F32)
+            longer = state * fade + ZB[s, j, 0:64, :].astype(F32)
             state = jnp.where(s < z, longer, state)
         halves.append(state)
+    halves = [jnp.concatenate(halves[j::2], axis=0) for j in range(2)]
     carried = jnp.concatenate(halves, axis=1).astype(BF)
 
     ones = jnp.ones((8, 256), BF)
@@ -499,7 +515,7 @@
         at = y if h == 0 else x
         total = LS[qh, at] + RD[qh, 0].astype(F32) + RD[qh, 1].astype(F32)
         rows = pl.ds(qh * 128, 128)
-        mine = G[y, x, k, pl.ds(HALO + qh * 128, 128), :].astype(F32)
+        mine = G[y, x, k, pl.ds(qh * 128, 128), :].astype(F32)
         res[rows, :] = (mine + total * scale[rows, :]).astype(BF)
         pltpu.make_async_copy(res.at[rows], out.at[rows], sems.at[5]).start()
 
@@ -631,13 +647,13 @@
             full(5, N, 256),
             full(ROWS, 256),
             full(ROWS, 256),
-            big(8, 2, N + 16, 128),
+            big(8, 4, 80, 128),
             big(ROWS, 128),
             dma(8),
             dma(NP, 5),
             dma(4),
             dma(4, 4),
-            dma(27),
+            dma(35),
         ],
         compiler_params=pltpu.CompilerParams(
             collective_id=0, has_side_effects=True, vmem_limit_bytes=VLIM

time: 98.7 us -> 97.6 us (0.989)
  Pallas kernels: 96.4 us -> 95.3 us
    pallas_call x1, Pallas kernels: 96.4 us -> 95.3 us  [local(): pl.pallas_call(layer_kernel, name='layer', out_shape=jax.ShapeDtypeStruct...]
where the time goes in v5:
time: 97.6 us; the launch traced here: 97 us
  Pallas kernels  95.3 us (98%)
  local copies, waits for them, and re-layouts  1.67 us (2%)
    pallas_call x1, Pallas kernels, local(): pl.pallas_call(layer_kernel, name='layer', out_shape=jax.ShapeDtypeStruct...  95.3 us

profile of v5, /device:TPU:2, one launch (start us, length us, event | category | flops | bytes accessed | tf_op | source)
XLA Modules:
  0.0 97.0 jit_solution(9970967479788263994)
XLA Ops:
  0.0 95.3 %layer.1 = bf16[1024,128]{1,0:T(8,128)(2,1)} custom-call(bf16[1024,128]{1,0:T(8,128)(2,1)} %tok.1, bf16[128,384]{1,0:T(8,128)(2,1)} %stp.1, f32[1,4096]{1,0:T(1,128)} %bitcast.2, bf16[4096,256]{1,0:T(8,128)(2,1)} %gate_hbm.1, bf16[4096,256]{1,0:T(8,128)(2,1)} %inner_hbm.1, f32[4,256]{1,0:T(4,128)} %cw.1, f32[4,256]{1,0:T(4,128)} %cs.1, f32[4]{0:T(128)} %log_rate.1, ...), custom_call_target="tpu_custom_call" | custom-call | tf_op jit(solution)/shard_map/layer/pallas_call | solution.py:612
  95.3 1.7 %copy.14 = bf16[1024,128]{1,0:T(8,128)(2,1)} copy(bf16[1024,128]{1,0:T(8,128)(2,1)} %layer.1) | data formatting | bytes 524288

commit v6 on v5

--- a/solution.py
+++ b/solution.py
@@ -202,11 +202,10 @@
         inv[rows, :] = lax.rsqrt(total * (1.0 / 4096) + 1e-05)
 
     def state_weights():
+        mine = pl.ds(pl.multiple_of(SBASE + k * 128, 16), 128)
         for c in range(32):
-            for j in range(3):
-                W[c * 128 : (c + 1) * 128, 512 + j * 128 : 640 + j * 128] = load_block(
-                    c, pl.ds(SBASE + j * 128, 128)
-                )
+            W[c * 128 : (c + 1) * 128, 512:640] = load_block(c, mine)
+            W[c * 128 : (c + 1) * 128, 640:768] = load_block(c, pl.ds(SBASE + 256, 128))
 
     def project_gate(q):
         rows = slice(q * Q, q * Q + Q)
@@ -221,16 +220,16 @@
 
     def project_state(q):
         rows = slice(q * Q, q * Q + Q)
-        raw = jnp.dot(X[rows, :], W[:, 512:896], preferred_element_type=F32) * inv[rows, :]
+        raw = jnp.dot(X[rows, :], W[:, 512:768], preferred_element_type=F32) * inv[rows, :]
         PJ[HALO + q * Q : HALO + q * Q + Q, :] = raw
 
     def project(q):
         first, count = span(q)
         rows = slice(first, first + count)
         to = slice(HALO + first, HALO + first + count) if q < 4 else slice(0, HALO)
-        raw = jnp.dot(X[rows, :], W[:, 256:896], preferred_element_type=F32) * inv[rows, :]
+        raw = jnp.dot(X[rows, :], W[:, 256:768], preferred_element_type=F32) * inv[rows, :]
         IN[to, :] = raw[:, 0:256].astype(BF)
-        PJ[to, :] = raw[:, 256:640]
+        PJ[to, :] = raw[:, 256:512]
 
     lane = lax.broadcasted_iota(jnp.int32, (1, 128), 1)
 
@@ -276,14 +275,19 @@
     BE[0] = jnp.zeros((8, 128), F32)
     tri = lower.astype(F32).astype(BF)
 
+    def maps(b):
+        rows = pl.ds(b * Q, Q)
+        taps = cs[:, pl.ds(pl.multiple_of(k * 128, 128), 128)]
+        BC[k, rows, :] = mix(PJ[pl.ds(b * Q, Q + HALO), 0:128], taps).astype(BF)
+        half = BC.at[k, rows]
+        remote(half, half, sems.at[35], sems.at[36 + b], sib).start()
+
     def states(b):
         r0 = b * Q
         rows = pl.ds(r0, Q)
         xs = mix(IN[pl.ds(r0, Q + HALO), :].astype(F32), cw[...])
         XC[rows, :] = xs
-        maps = mix(PJ[pl.ds(r0, Q + HALO), 0:256], cs[...]).astype(BF)
-        BC[rows, :] = maps
-        rate = pltpu.roll(PJ[pl.ds(r0 + HALO, Q), 256:384], shift, 1)
+        rate = pltpu.roll(PJ[pl.ds(r0 + HALO, Q), 128:256], shift, 1)
         step = softplus(rate + bias_row)
         decay = rate_row * step
         within = jnp.zeros((Q, 128), F32)
@@ -294,8 +298,10 @@
         last = within[Q - 1 : Q, :]
         BE[b + 1] = BE[b] + last
         weighted = (xs * wide(jnp.exp(last - within) * step)).astype(BF)
+        theirs = BC.at[0, rows]
+        remote(theirs, theirs, sems.at[35], sems.at[36 + b], sib).wait_recv()
         fresh = lax.dot_general(
-            maps[:, 0:N], weighted, (((0,), (0,)), ((), ())), preferred_element_type=F32
+            BC[0, rows, :], weighted, (((0,), (0,)), ((), ())), preferred_element_type=F32
         )
         SE[b + 1] = wide(jnp.exp(last)) * SE[b] + fresh
 
@@ -303,7 +309,7 @@
         rows = pl.ds(b * Q, Q)
         xs = XC[rows, :]
         xb = xs.astype(BF)
-        im, om = BC[rows, 0:N], BC[rows, N:]
+        im, om = BC[0, rows, :], BC[1, rows, :]
         within, step = WI[rows, :], DT[rows, :]
         scores = lax.dot_general(om, im, (((1,), (1,)), ((), ())), preferred_element_type=F32)
         within_t, step_t = within.T, step.T
@@ -384,12 +390,12 @@
             outp.at[:, pl.ds(col, 128)], Wo.at[pl.ds(256, 256), at], sems.at[11], sems.at[12], sib
         ).start()
 
-    GATE, FIRST, SW, AS, PR, ST, PF, PS = 5, 6, 7, 8, 9, 10, 11, 12
+    FIRST, SW, AS, PR, ST, PF, PS, MAPS = 5, 6, 7, 8, 9, 10, 11, 12
     for name, i in (
         (1, 0), (FIRST, 0), (1, 1), (2, 0), (1, 2), (2, 1), (1, 3), (1, 4),
         (3, 0), (2, 2), (3, 1), (2, 3), (4, 0), (AS, 0), (PF, 0), (3, 2), (2, 4), (4, 1),
-        (SW, 0), (AS, 4), (PR, 4), (PS, 0), (3, 3), (4, 2), (ST, 0), (AS, 1), (3, 4), (PR, 1), (4, 3), (ST, 1),
-        (AS, 2), (4, 4), (PR, 2), (ST, 2), (AS, 3), (PR, 3), (ST, 3),
+        (SW, 0), (AS, 4), (PR, 4), (PS, 0), (MAPS, 0), (3, 3), (4, 2), (AS, 1), (ST, 0), (3, 4), (PR, 1), (MAPS, 1),
+        (4, 3), (AS, 2), (ST, 1), (4, 4), (PR, 2), (MAPS, 2), (AS, 3), (ST, 2), (PR, 3), (MAPS, 3), (ST, 3),
     ):
         if name == SW:
             t5(1)
@@ -402,8 +408,8 @@
                 if i == 0:
                     pltpu.make_async_copy(W.at[:, 0:512], W.at[:, 0:512], sems.at[4]).wait()
             (
-                t0, t1, t2, t3, t4, project_gate, None, None, assemble, project, states,
-                project_first, project_state,
+                t0, t1, t2, t3, t4, None, None, assemble, project, states,
+                project_first, project_state, maps,
             )[name](i)
 
     def zsteps(s):
@@ -441,7 +447,7 @@
 
     def finish(q):
         rows = pl.ds(q * Q, Q)
-        v = Y[rows, :] + jnp.dot(BC[rows, N:], carried, preferred_element_type=F32) * EG[rows, :]
+        v = Y[rows, :] + jnp.dot(BC[1, rows, :], carried, preferred_element_type=F32) * EG[rows, :]
         g[0, rows, :] = (v * gain[...]).astype(BF)
         remote(g.at[0, rows], g.at[1, rows], sems.at[6], sems.at[7 + q], sib).start()
         total = jnp.zeros((8, Q), F32)
@@ -584,6 +590,7 @@
     sent(half, sems.at[11])
     sent(ZB.at[pl.ds(0, 7)], sems.at[18])
     sent(g.at[0], sems.at[6])
+    sent(BC.at[0], sems.at[35])
     sent(ER.at[pl.ds(0, 7), one], sems.at[14])
     for stage, buf in enumerate((SA, SB, SC, SD)):
         sent(buf, send.at[stage])
@@ -618,11 +625,11 @@
         scratch_shapes=[
             big(4, 4, 2, GROWS, 128),
             big(ROWS + HALO, 4096),
-            big(4096, 896),
+            big(4096, 768),
             full(ROWS + HALO, 128),
             full(ROWS + HALO, 1),
             big(ROWS + HALO, 256),
-            full(ROWS + HALO, SROWS),
+            full(ROWS + HALO, 256),
             big(ROWS, 256),
             big(2, ROWS, 256),
             big(512, 2048),
@@ -640,7 +647,7 @@
             full(7, 8, ROWS),
             full(ROWS, 128),
             full(ROWS, 256),
-            big(ROWS, 256),
+            big(2, ROWS, 128),
             full(ROWS, 128),
             full(ROWS, 128),
             full(5, 8, 128),
@@ -653,7 +660,7 @@
             dma(NP, 5),
             dma(4),
             dma(4, 4),
-            dma(35),
+            dma(40),
         ],
         compiler_params=pltpu.CompilerParams(
             collective_id=0, has_side_effects=True, vmem_limit_bytes=VLIM

time: 97.6 us -> 98.2 us (level)
  no operation moved by 1% of the time
where the time goes in v6:
time: 98.2 us; the launch traced here: 97.7 us
  Pallas kernels  96 us (98%)
  local copies, waits for them, and re-layouts  1.67 us (2%)
    pallas_call x1, Pallas kernels, local(): pl.pallas_call(layer_kernel, name='layer', out_shape=jax.ShapeDtypeStruct...  96 us

profile of v6, /device:TPU:2, one launch (start us, length us, event | category | flops | bytes accessed | tf_op | source)
XLA Modules:
  0.0 97.7 jit_solution(13782075306013720040)
XLA Ops:
  0.0 96.0 %layer.1 = bf16[1024,128]{1,0:T(8,128)(2,1)} custom-call(bf16[1024,128]{1,0:T(8,128)(2,1)} %tok.1, bf16[128,384]{1,0:T(8,128)(2,1)} %stp.1, f32[1,4096]{1,0:T(1,128)} %bitcast.2, bf16[4096,256]{1,0:T(8,128)(2,1)} %gate_hbm.1, bf16[4096,256]{1,0:T(8,128)(2,1)} %inner_hbm.1, f32[4,256]{1,0:T(4,128)} %cw.1, f32[4,256]{1,0:T(4,128)} %cs.1, f32[4]{0:T(128)} %log_rate.1, ...), custom_call_target="tpu_custom_call" | custom-call | tf_op jit(solution)/shard_map/layer/pallas_call | solution.py:619
  96.0 1.7 %copy.14 = bf16[1024,128]{1,0:T(8,128)(2,1)} copy(bf16[1024,128]{1,0:T(8,128)(2,1)} %layer.1) | data formatting | bytes 524288

commit v7 on v6

--- a/solution.py
+++ b/solution.py
@@ -394,8 +394,8 @@
     for name, i in (
         (1, 0), (FIRST, 0), (1, 1), (2, 0), (1, 2), (2, 1), (1, 3), (1, 4),
         (3, 0), (2, 2), (3, 1), (2, 3), (4, 0), (AS, 0), (PF, 0), (3, 2), (2, 4), (4, 1),
-        (SW, 0), (AS, 4), (PR, 4), (PS, 0), (MAPS, 0), (3, 3), (4, 2), (AS, 1), (ST, 0), (3, 4), (PR, 1), (MAPS, 1),
-        (4, 3), (AS, 2), (ST, 1), (4, 4), (PR, 2), (MAPS, 2), (AS, 3), (ST, 2), (PR, 3), (MAPS, 3), (ST, 3),
+        (SW, 0), (AS, 4), (PR, 4), (PS, 0), (MAPS, 0), (3, 3), (4, 2), (ST, 0), (AS, 1), (3, 4), (PR, 1), (MAPS, 1),
+        (4, 3), (ST, 1), (AS, 2), (4, 4), (PR, 2), (MAPS, 2), (ST, 2), (AS, 3), (PR, 3), (MAPS, 3), (ST, 3),
     ):
         if name == SW:
             t5(1)
@@ -558,6 +558,7 @@
     remote(half, half, sems.at[11], sems.at[12], sib).wait_recv()
     finish(0)
     finish(1)
+    finish(2)
     for q in range(4):
         theirs = g.at[1, pl.ds(q * Q, Q)]
         remote(theirs, theirs, sems.at[6], sems.at[7 + q], sib).wait_recv()
@@ -565,9 +566,8 @@
             energy(0)
         u0(2 * q)
         u0(2 * q + 1)
-        if q < 2:
-            finish(q + 2)
-        if q == 1:
+        if q == 0:
+            finish(3)
             remote(EO.at[0, one], ER.at[0, one], sems.at[14], sems.at[15], sib).start()
     for name, q in (
         (1, 0), (1, 1), (5, 1), (1, 2), (1, 3), (2, 0), (2, 1), (5, 2), (2, 2), (2, 3),

time: 98.2 us -> 97.2 us (0.990)
  no operation moved by 1% of the time
where the time goes in v7:
time: 97.2 us; the launch traced here: 96.9 us
  Pallas kernels  95.2 us (98%)
  local copies, waits for them, and re-layouts  1.67 us (2%)
    pallas_call x1, Pallas kernels, local(): pl.pallas_call(layer_kernel, name='layer', out_shape=jax.ShapeDtypeStruct...  95.2 us

profile of v7, /device:TPU:2, one launch (start us, length us, event | category | flops | bytes accessed | tf_op | source)
XLA Modules:
  0.0 96.9 jit_solution(12888713522269336930)
XLA Ops:
  0.0 95.2 %layer.1 = bf16[1024,128]{1,0:T(8,128)(2,1)} custom-call(bf16[1024,128]{1,0:T(8,128)(2,1)} %tok.1, bf16[128,384]{1,0:T(8,128)(2,1)} %stp.1, f32[1,4096]{1,0:T(1,128)} %bitcast.2, bf16[4096,256]{1,0:T(8,128)(2,1)} %gate_hbm.1, bf16[4096,256]{1,0:T(8,128)(2,1)} %inner_hbm.1, f32[4,256]{1,0:T(4,128)} %cw.1, f32[4,256]{1,0:T(4,128)} %cs.1, f32[4]{0:T(128)} %log_rate.1, ...), custom_call_target="tpu_custom_call" | custom-call | tf_op jit(solution)/shard_map/layer/pallas_call | solution.py:619
  95.2 1.7 %copy.14 = bf16[1024,128]{1,0:T(8,128)(2,1)} copy(bf16[1024,128]{1,0:T(8,128)(2,1)} %layer.1) | data formatting | bytes 524288
